TPU v7x, 16 devices: a whole 2x2x2 slice. The times are simulated.
16 devices in a mesh: prob: 4 (over z, y), feat: 4 (over x, core).
Axes of the slice: x: 2, y: 2, z: 2, core: 2. Of those that a mesh axis runs over, the one named last changes fastest.
Arguments:
- design: bfloat16 [65536, 2048], P('prob', 'feat'), parts along dimension 0
- coef_init: float32 [8192, 8], P(('prob', 'feat')), parts along dimension 0
- targets: float32 [65536, 8], P('prob'), parts along dimension 0
- step_sizes: float32 [8192], P(('prob', 'feat')), parts along dimension 0
Outputs:
- output 1: float32 [8192, 8], P(('prob', 'feat')), parts along dimension 0
- output 2: float32 [65536, 8], P('prob'), parts along dimension 0
There are 4 independent parts. A program takes and returns all parts, laid end to end along the dimension named above; each array names one.
All inputs are finite; a program needn't handle non-finite values.
Results may differ from a plain program's by a relative error of at most 0.0057789.
Values are sent between devices in bfloat16 or wider.
A program may use at most 1 GiB of HBM per device.

v0:
```python
import jax
import jax.numpy as jnp
from jax import lax
from jax.sharding import PartitionSpec as P

SWEEPS = 6
COMBINE_WEIGHT = 0.8


def solution(mesh):
    group_size = mesh.shape['feat']

    def local_run(x_local, coef_local, targets_local, step_local):
        samples = x_local.shape[0]
        features = x_local.shape[1] * group_size
        lasso_weight = 0.3 * group_size / features ** 0.5
        step_col = step_local[:, None]
        thresholds = step_col * lasso_weight

        def summed_product(values):
            product = jnp.dot(x_local, values.astype(jnp.bfloat16), preferred_element_type=jnp.float32)
            return lax.psum(product.astype(jnp.bfloat16).astype(jnp.float32), 'feat')

        weights = coef_local
        residual = targets_local - summed_product(weights)
        for _ in range(SWEEPS):
            gradient = lax.dot_general(x_local, residual.astype(jnp.bfloat16), (((0,), (0,)), ((), ())), preferred_element_type=jnp.float32) / samples
            stepped = weights + step_col * gradient
            shrunk = jnp.sign(stepped) * jnp.maximum(jnp.abs(stepped) - thresholds, 0.0)
            change = shrunk - weights
            weights = weights + COMBINE_WEIGHT * change
            residual = residual - COMBINE_WEIGHT * summed_product(change)
        return weights, residual

    return jax.shard_map(local_run, mesh=mesh, in_specs=(P('prob', 'feat'), P(('prob', 'feat'), None), P('prob', None), P(('prob', 'feat'))), out_specs=(P(('prob', 'feat'), None), P('prob', None)), check_vma=False)
```

profile of v0, /device:TPU:0, one launch (start us, length us, event | category | flops | bytes accessed | tf_op | source)
XLA Modules:
  0.0 357.0 jit_solution(18241428130174005698)
XLA Ops:
  7.2 0.0 copy-start.4
  7.2 0.0 copy-start.5
  7.2 0.0 copy-start.3
  7.2 0.0 all-reduce.8.cloned.1.call-start
  7.2 11.0 %fusion.12 = f32[16384,8]{0,1:T(8,128)} fusion(bf16[16384,512]{1,0:T(8,128)(2,1)} %param.4, f32[512,8]{0,1:T(8,128)} %param.5), kind=kOutput, calls=%fused_computation.19 | convolution fusion | flops 134483968 | bytes 17317888 | tf_op jit(solution)/shard_map/dot_general | solution.py:21
  18.3 0.0 all-reduce.8.cloned.1.call-update
  18.3 0.0 all-reduce.10.cloned.1.call-start
  18.4 0.0 copy-done.5
  18.4 32.5 %all-reduce.8.cloned.1.call-done = f32[16384,8]{0,1:T(8,128)} async-done(((f32[16384,8]{0,1:T(8,128)}), f32[16384,8]{0,1:T(8,128)}) %all-reduce.8.cloned.1.call-update) | async-done | bytes 524304 | tf_op jit(solution)/shard_map/psum | solution.py:22
  50.8 0.0 copy-done.3
  50.9 1.1 sub.77
  52.0 0.0 copy-done.4
  52.0 8.0 %multiply_subtract_fusion.14 = f32[512,8]{0,1:T(8,128)S(1)} fusion(f32[512,8]{0,1:T(8,128)S(1)} %copy-done.4, bf16[16384,512]{1,0:T(8,128)(2,1)} %param.4, f32[16384,8]{0,1:T(8,128)S(1)} %sub.77, f32[512]{0:T(512)S(1)} %get-tuple-element.3, f32[512]{0:T(512)S(1)} %get-tuple-element.2), kind=kOutput, calls=%fused_computation.61 | convolution fusion | flops 134381568 | bytes 17338368 | tf_op jit(solution)/shard_map/dot_general | solution.py:27
  60.0 11.0 %fusion.11 = f32[16384,8]{0,1:T(8,128)} fusion(bf16[16384,512]{1,0:T(8,128)(2,1)} %param.4, f32[512,8]{0,1:T(8,128)S(1)} %multiply_subtract_fusion.14), kind=kOutput, calls=%fused_computation.17 | convolution fusion | flops 134483968 | bytes 17317888 | tf_op jit(solution)/shard_map/dot_general | solution.py:21
  71.0 0.0 all-reduce.10.cloned.1.call-update
  71.0 0.0 all-reduce.12.cloned.1.call-start
  71.1 29.7 %all-reduce.10.cloned.1.call-done = f32[16384,8]{0,1:T(8,128)} async-done(((f32[16384,8]{0,1:T(8,128)}), f32[16384,8]{0,1:T(8,128)}) %all-reduce.10.cloned.1.call-update) | async-done | bytes 524304 | tf_op jit(solution)/shard_map/psum | solution.py:22
  100.8 0.0 copy-start.2
  100.8 8.3 %multiply_add_fusion.4 = (f32[512,8]{0,1:T(8,128)S(1)}, bf16[512,8]{0,1:T(8,128)(2,1)S(1)}) fusion(f32[512,8]{0,1:T(8,128)S(1)} %copy-done.4, f32[512,8]{0,1:T(8,128)S(1)} %multiply_subtract_fusion.14, f32[512]{0:T(512)S(1)} %get-tuple-element.3, f32[512]{0:T(512)S(1)} %get-tuple-element.2, bf16[16384,512]{1,0:T(8,128)(2,1)} %param.4, ...), kind=kOutput, calls=%fused_computation.58 | convolution fusion | flops 134664192 | bytes 17887232 | tf_op jit(solution)/shard_map/dot_general | solution.py:27
  109.0 11.0 %fusion.9 = f32[16384,8]{0,1:T(8,128)} fusion(bf16[16384,512]{1,0:T(8,128)(2,1)} %param.4, bf16[512,8]{0,1:T(8,128)(2,1)S(1)} %get-tuple-element.5), kind=kOutput, calls=%fused_computation.14 | convolution fusion | flops 134479872 | bytes 17309696 | tf_op jit(solution)/shard_map/dot_general | solution.py:21
  120.0 0.0 all-reduce.12.cloned.1.call-update
  120.0 0.2 all-reduce.14.cloned.1.call-start
  120.3 29.5 %all-reduce.12.cloned.1.call-done = f32[16384,8]{0,1:T(8,128)} async-done(((f32[16384,8]{0,1:T(8,128)}), f32[16384,8]{0,1:T(8,128)}) %all-reduce.12.cloned.1.call-update) | async-done | bytes 524304 | tf_op jit(solution)/shard_map/psum | solution.py:22
  149.8 0.0 copy-done.2
  149.8 1.1 multiply_subtract_fusion.4
  150.9 8.0 %multiply_subtract_fusion.12 = f32[512,8]{0,1:T(8,128)S(1)} fusion(f32[512,8]{0,1:T(8,128)S(1)} %get-tuple-element.4, bf16[16384,512]{1,0:T(8,128)(2,1)} %param.4, f32[16384,8]{0,1:T(8,128)S(1)} %multiply_subtract_fusion.4, f32[512]{0:T(512)S(1)} %get-tuple-element.3, f32[512]{0:T(512)S(1)} %get-tuple-element.2), kind=kOutput, calls=%fused_computation.57 | convolution fusion | flops 134381568 | bytes 17338368 | tf_op jit(solution)/shard_map/dot_general | solution.py:27
  159.0 11.0 %fusion.7 = f32[16384,8]{0,1:T(8,128)} fusion(bf16[16384,512]{1,0:T(8,128)(2,1)} %param.4, f32[512,8]{0,1:T(8,128)S(1)} %multiply_subtract_fusion.12), kind=kOutput, calls=%fused_computation.11 | convolution fusion | flops 134483968 | bytes 17317888 | tf_op jit(solution)/shard_map/dot_general | solution.py:21
  170.0 0.0 all-reduce.14.cloned.1.call-update
  170.0 0.0 all-reduce.16.cloned.1.call-start
  170.0 29.7 %all-reduce.14.cloned.1.call-done = f32[16384,8]{0,1:T(8,128)} async-done(((f32[16384,8]{0,1:T(8,128)}), f32[16384,8]{0,1:T(8,128)}) %all-reduce.14.cloned.1.call-update) | async-done | bytes 524304 | tf_op jit(solution)/shard_map/psum | solution.py:22
  199.7 0.0 copy-start
  199.7 8.3 %multiply_add_fusion.2 = (f32[512,8]{0,1:T(8,128)S(1)}, bf16[512,8]{0,1:T(8,128)(2,1)S(1)}) fusion(f32[512,8]{0,1:T(8,128)S(1)} %get-tuple-element.4, f32[512,8]{0,1:T(8,128)S(1)} %multiply_subtract_fusion.12, f32[512]{0:T(512)S(1)} %get-tuple-element.3, f32[512]{0:T(512)S(1)} %get-tuple-element.2, bf16[16384,512]{1,0:T(8,128)(2,1)} %param.4, ...), kind=kOutput, calls=%fused_computation.54 | convolution fusion | flops 134664192 | bytes 17887232 | tf_op jit(solution)/shard_map/dot_general | solution.py:27
  208.0 11.0 %fusion.5 = f32[16384,8]{0,1:T(8,128)} fusion(bf16[16384,512]{1,0:T(8,128)(2,1)} %param.4, bf16[512,8]{0,1:T(8,128)(2,1)S(1)} %get-tuple-element.7), kind=kOutput, calls=%fused_computation.8 | convolution fusion | flops 134479872 | bytes 17309696 | tf_op jit(solution)/shard_map/dot_general | solution.py:21
  219.0 0.0 all-reduce.16.cloned.1.call-update
  219.0 0.0 all-reduce.18.cloned.1.call-start
  219.0 29.7 %all-reduce.16.cloned.1.call-done = f32[16384,8]{0,1:T(8,128)} async-done(((f32[16384,8]{0,1:T(8,128)}), f32[16384,8]{0,1:T(8,128)}) %all-reduce.16.cloned.1.call-update) | async-done | bytes 524304 | tf_op jit(solution)/shard_map/psum | solution.py:22
  248.7 0.0 copy-done
  248.7 1.1 multiply_subtract_fusion.2
  249.9 8.0 %multiply_subtract_fusion.10 = f32[512,8]{0,1:T(8,128)S(1)} fusion(f32[512,8]{0,1:T(8,128)S(1)} %get-tuple-element.6, bf16[16384,512]{1,0:T(8,128)(2,1)} %param.4, f32[16384,8]{0,1:T(8,128)S(1)} %multiply_subtract_fusion.2, f32[512]{0:T(512)S(1)} %get-tuple-element.3, f32[512]{0:T(512)S(1)} %get-tuple-element.2), kind=kOutput, calls=%fused_computation.53 | convolution fusion | flops 134381568 | bytes 17338368 | tf_op jit(solution)/shard_map/dot_general | solution.py:27
  257.9 11.0 %fusion.3 = f32[16384,8]{0,1:T(8,128)} fusion(bf16[16384,512]{1,0:T(8,128)(2,1)} %param.4, f32[512,8]{0,1:T(8,128)S(1)} %multiply_subtract_fusion.10), kind=kOutput, calls=%fused_computation.5 | convolution fusion | flops 134483968 | bytes 17317888 | tf_op jit(solution)/shard_map/dot_general | solution.py:21
  268.9 0.0 all-reduce.18.cloned.1.call-update
  268.9 0.3 all-reduce.20.cloned.1.call-start
  269.2 29.4 %all-reduce.18.cloned.1.call-done = f32[16384,8]{0,1:T(8,128)} async-done(((f32[16384,8]{0,1:T(8,128)}), f32[16384,8]{0,1:T(8,128)}) %all-reduce.18.cloned.1.call-update) | async-done | bytes 524304 | tf_op jit(solution)/shard_map/psum | solution.py:22
  298.6 0.0 copy-start.1
  298.6 8.9 %multiply_add_fusion = (f32[512,8]{0,1:T(8,128)}, bf16[512,8]{0,1:T(8,128)(2,1)S(1)}) fusion(f32[512,8]{0,1:T(8,128)S(1)} %get-tuple-element.6, f32[512,8]{0,1:T(8,128)S(1)} %multiply_subtract_fusion.10, f32[512]{0:T(512)S(1)} %get-tuple-element.3, f32[512]{0:T(512)S(1)} %get-tuple-element.2, bf16[16384,512]{1,0:T(8,128)(2,1)} %param.4, ...), kind=kOutput, calls=%fused_computation.50 | convolution fusion | flops 134664192 | bytes 17887232 | tf_op jit(solution)/shard_map/dot_general | solution.py:27
  307.5 11.0 %fusion.1 = f32[16384,8]{0,1:T(8,128)} fusion(bf16[16384,512]{1,0:T(8,128)(2,1)} %param.4, bf16[512,8]{0,1:T(8,128)(2,1)S(1)} %get-tuple-element.9), kind=kOutput, calls=%fused_computation.2 | convolution fusion | flops 134479872 | bytes 17309696 | tf_op jit(solution)/shard_map/dot_general | solution.py:21
  318.5 0.0 all-reduce.20.cloned.1.call-update
  318.5 29.7 %all-reduce.20.cloned.1.call-done = f32[16384,8]{0,1:T(8,128)} async-done(((f32[16384,8]{0,1:T(8,128)}), f32[16384,8]{0,1:T(8,128)}) %all-reduce.20.cloned.1.call-update) | async-done | bytes 524304 | tf_op jit(solution)/shard_map/psum | solution.py:22
  348.3 0.0 copy-done.1
  348.3 1.9 multiply_subtract_fusion
  (1 shorter events, 0.0 us)
Async XLA Ops:
  7.2 44.8 %copy-start.4 = (f32[512,8]{0,1:T(8,128)S(1)}, f32[512,8]{0,1:T(8,128)}, u32[]{:S(2)}) copy-start(f32[512,8]{0,1:T(8,128)} %param.5) | copy-start | bytes 49156
  7.2 11.2 %copy-start.5 = (f32[512]{0:T(512)S(1)}, f32[512]{0:T(512)}, u32[]{:S(2)}) copy-start(f32[512]{0:T(512)} %param.7) | copy-start | bytes 6148
  7.2 43.7 %copy-start.3 = (f32[16384,8]{0,1:T(8,128)S(1)}, f32[16384,8]{0,1:T(8,128)}, u32[]{:S(2)}) copy-start(f32[16384,8]{0,1:T(8,128)} %param.6) | copy-start | bytes 1572868
  7.2 43.7 %all-reduce.8.cloned.1.call-start = ((), (), s32[]{:S(2)}) async-start(), calls=%async_computation | async-start | bytes 1048576 | tf_op jit(solution)/shard_map/psum | solution.py:22
  18.3 82.4 %all-reduce.10.cloned.1.call-start = ((), (), s32[]{:S(2)}) async-start(), calls=%async_computation.1 | async-start | bytes 1048576 | tf_op jit(solution)/shard_map/psum | solution.py:22
  71.0 78.7 %all-reduce.12.cloned.1.call-start = ((), (), s32[]{:S(2)}) async-start(), calls=%async_computation.2 | async-start | bytes 1048576 | tf_op jit(solution)/shard_map/psum | solution.py:22
  100.8 49.0 %copy-start.2 = (f32[16384,8]{0,1:T(8,128)S(1)}, f32[16384,8]{0,1:T(8,128)}, u32[]{:S(2)}) copy-start(f32[16384,8]{0,1:T(8,128)} %all-reduce.10.cloned.1.call-done) | copy-start | bytes 1572868
  120.0 79.7 %all-reduce.14.cloned.1.call-start = ((), (), s32[]{:S(2)}) async-start(), calls=%async_computation.3 | async-start | bytes 1048576 | tf_op jit(solution)/shard_map/psum | solution.py:22
  170.0 78.7 %all-reduce.16.cloned.1.call-start = ((), (), s32[]{:S(2)}) async-start(), calls=%async_computation.4 | async-start | bytes 1048576 | tf_op jit(solution)/shard_map/psum | solution.py:22
  199.7 49.0 %copy-start = (f32[16384,8]{0,1:T(8,128)S(1)}, f32[16384,8]{0,1:T(8,128)}, u32[]{:S(2)}) copy-start(f32[16384,8]{0,1:T(8,128)} %all-reduce.14.cloned.1.call-done) | copy-start | bytes 1572868
  219.0 79.7 %all-reduce.18.cloned.1.call-start = ((), (), s32[]{:S(2)}) async-start(), calls=%async_computation.5 | async-start | bytes 1048576 | tf_op jit(solution)/shard_map/psum | solution.py:22
  268.9 79.3 %all-reduce.20.cloned.1.call-start = ((), (), s32[]{:S(2)}) async-start(), calls=%async_computation.6 | async-start | bytes 1048576 | tf_op jit(solution)/shard_map/psum | solution.py:22
  298.6 49.6 %copy-start.1 = (f32[16384,8]{0,1:T(8,128)S(1)}, f32[16384,8]{0,1:T(8,128)}, u32[]{:S(2)}) copy-start(f32[16384,8]{0,1:T(8,128)} %all-reduce.18.cloned.1.call-done) | copy-start | bytes 1572868
Sparse Core Ops, SparseCore 0:
  18.4 32.3 all-reduce.7
  71.2 29.5 all-reduce.9
  120.2 29.5 all-reduce.11
  170.1 29.5 all-reduce.13
  219.1 29.5 all-reduce.15
  269.0 29.5 all-reduce.17
  318.7 29.5 all-reduce.19
where the time goes:
time: 358 us; the launch traced here: 357 us
  waiting for transfers between devices  210 us (59%)
  matrix products  127 us (35%)
  between operations  14.2 us (4%)
  other arithmetic  5.3 us (1%)
    psum x7, waiting for transfers between devices, summed_product(): return lax.psum(product.astype(jnp.bfloat16).astype(jnp.float32), 'feat')  210 us
    dot_general x7, matrix products, summed_product(): jnp.dot(x_local, values.astype(jnp.bfloat16), preferred_element_type=jnp....  77 us
    dot_general x6, matrix products, local_run(): lax.dot_general(x_local, residual.astype(jnp.bfloat16), (((0,), (0,)), ((...  49.6 us
  transfers between devices with their start and end apart: 7, of which 7 were waited for; matrix products, arithmetic and copies ran while one was open for 0% of the time, Pallas kernels for 0%

commit v1 on v0

v1 whole, which is shorter than its diff:
```python
import functools

import jax
import jax.numpy as jnp
from jax import lax
from jax.experimental import pallas as pl
from jax.experimental.pallas import tpu as pltpu
from jax.sharding import PartitionSpec as P

SWEEPS = 6
COMBINE_WEIGHT = 0.8
EXPLICIT = False
LAG = 3
TILE = 256
MESH = pl.DeviceIdType.MESH
OWN, PARTNER, CROSS, RELAYED = 0, 1, 2, 3


def chunk_list(samples):
    size = samples // 16
    return [(i * size, size) for i in range(16)]


def kernel(chunks, lasso_weight, samples, *refs):
    (x_hbm, w0_ref, y_hbm, eta_ref, w_out, r_out, xv, rv, ubuf, wv, dwv, gv, x_sem, y_sem, out_sem,
     own_send, cross_send, relay_send, own_recv, cross_recv, relay_recv) = refs
    count = len(chunks)
    targets, features = w0_ref.shape
    depth_tiles = features // TILE
    me = lax.axis_index('feat')
    partner = me + 1 - 2 * lax.rem(me, 2)
    cross = 3 - me

    def rows_of(c):
        start, size = chunks[c]
        return pl.ds(start, size)

    def x_copy(c):
        return pltpu.make_async_copy(x_hbm.at[rows_of(c)], xv.at[rows_of(c)], x_sem.at[c])

    def remote(par, c, src, dst, peer, send_sem, recv_sem):
        return pltpu.make_async_remote_copy(
            src_ref=ubuf.at[par, src, :, rows_of(c)], dst_ref=ubuf.at[par, dst, :, rows_of(c)],
            send_sem=send_sem.at[par, c], recv_sem=recv_sem.at[par, c], device_id={'feat': peer}, device_id_type=MESH)

    def own_copy(par, c):
        return remote(par, c, OWN, PARTNER, partner, own_send, own_recv)

    def cross_copy(par, c):
        return remote(par, c, OWN, CROSS, cross, cross_send, cross_recv)

    def relay_copy(par, c):
        return remote(par, c, CROSS, RELAYED, partner, relay_send, relay_recv)

    def body(*accs):
        forward_acc = [accs[:len(accs) // 2 - 1], accs[len(accs) // 2:-1]]
        gradient_acc = [accs[len(accs) // 2 - 1], accs[-1]]

        def tiles_of(c):
            start, size = chunks[c]
            return [start + i * TILE for i in range(size // TILE)]

        def acc_of(c, i):
            half = len(forward_acc[0]) // 2
            return forward_acc[i % 2][(c % 2) * half + i // 2]

        def issue_forward(c):
            if not EXPLICIT:
                return
            change = [dwv[:, kt * TILE:(kt + 1) * TILE] for kt in range(depth_tiles)]
            for i, row in enumerate(tiles_of(c)):
                for kt in range(depth_tiles):
                    pltpu.matmul_push_rhs(xv[pl.ds(row, TILE), pl.ds(kt * TILE, TILE)], staging_register=kt % 2, mxu_index=i % 2, transpose=True)
                    pltpu.matmul_acc_lhs(acc_of(c, i), change[kt], load_staged_rhs=kt % 2)

        def collect_forward(par, c):
            for i, row in enumerate(tiles_of(c)):
                if EXPLICIT:
                    product = pltpu.matmul_pop(acc_of(c, i))
                else:
                    product = lax.dot_general(dwv[...].astype(jnp.bfloat16), xv[pl.ds(row, TILE), :], (((1,), (1,)), ((), ())), preferred_element_type=jnp.float32)
                ubuf[par, OWN, :, pl.ds(row, TILE)] = product.astype(jnp.bfloat16)

        def issue_gradient(c):
            for row in tiles_of(c):
                lhs = rv[:, pl.ds(row, TILE)].astype(jnp.bfloat16).astype(jnp.float32)
                for q in range(depth_tiles):
                    x_tile = xv[pl.ds(row, TILE), pl.ds(q * TILE, TILE)]
                    if EXPLICIT:
                        pltpu.matmul_push_rhs(x_tile, staging_register=(row // TILE) % 2, mxu_index=q)
                        pltpu.matmul_acc_lhs(gradient_acc[q], lhs, load_staged_rhs=(row // TILE) % 2)
                    else:
                        gv[:, pl.ds(q * TILE, TILE)] += jnp.dot(lhs.astype(jnp.bfloat16), x_tile, preferred_element_type=jnp.float32)

        def update_weights():
            for q in range(depth_tiles):
                cols = pl.ds(q * TILE, TILE)
                if EXPLICIT:
                    gradient = pltpu.matmul_pop(gradient_acc[q])
                else:
                    gradient = gv[:, cols]
                    gv[:, cols] = jnp.zeros_like(gradient)
                eta = jnp.broadcast_to(eta_ref[:, cols], (targets, TILE))
                threshold = eta * lasso_weight
                weights = wv[:, cols]
                stepped = weights + eta * (gradient * (1.0 / samples))
                shrunk = jnp.where(stepped > threshold, stepped - threshold, jnp.where(stepped < -threshold, stepped + threshold, 0.0))
                change = shrunk - weights
                wv[:, cols] = weights + COMBINE_WEIGHT * change
                dwv[:, cols] = change.astype(jnp.bfloat16).astype(jnp.float32)

        def wait_sends(par):
            for c in range(count):
                own_copy(par, c).wait_send()
                cross_copy(par, c).wait_send()
                relay_copy(par, c).wait_send()

        def phase(par, first=False, last=False):
            def send(c):
                collect_forward(par, c)
                cross_copy(par, c).start()
                own_copy(par, c).start()

            for c in range(count):
                if first:
                    x_copy(c).wait()
                issue_forward(c)
                if c > 0:
                    send(c - 1)
                if c == count // 2 and not first:
                    wait_sends(1 - par)
            send(count - 1)
            if first:
                pltpu.make_async_copy(y_hbm, rv, y_sem).wait()
            for step in range(count + LAG):
                if step < count:
                    cross_copy(par, step).wait_recv()
                    relay_copy(par, step).start()
                c = step - LAG
                if c < 0:
                    continue
                own_copy(par, c).wait_recv()
                relay_copy(par, c).wait_recv()
                for row in tiles_of(c):
                    cols = pl.ds(row, TILE)
                    u = [ubuf[par, slot, :, cols].astype(jnp.float32) for slot in range(4)]
                    total = (u[OWN] + u[PARTNER]) + (u[CROSS] + u[RELAYED])
                    rv[:, cols] = rv[:, cols] - (total if first else COMBINE_WEIGHT * total)
                if last:
                    pltpu.make_async_copy(rv.at[:, rows_of(c)], r_out.at[:, rows_of(c)], out_sem.at[c]).start()
                else:
                    issue_gradient(c)
            if not last:
                update_weights()

        phase(0, first=True)

        def sweep(s, carry):
            phase(lax.rem(s, 2))
            return carry

        lax.fori_loop(1, SWEEPS, sweep, 0)
        phase(SWEEPS % 2, last=True)
        w_out[...] = wv[...]
        wait_sends(SWEEPS % 2)
        for c in range(count):
            pltpu.make_async_copy(rv.at[:, rows_of(c)], r_out.at[:, rows_of(c)], out_sem.at[c]).wait()

    for c in range(count):
        x_copy(c).start()
        if c == 0:
            pltpu.make_async_copy(y_hbm, rv, y_sem).start()
    barrier = pltpu.get_barrier_semaphore()
    for peer in (partner, cross):
        pl.semaphore_signal(barrier, inc=1, device_id={'feat': peer}, device_id_type=MESH)
    wv[...] = w0_ref[...]
    dwv[...] = w0_ref[...].astype(jnp.bfloat16).astype(jnp.float32)
    if not EXPLICIT:
        gv[...] = jnp.zeros_like(gv)
    pl.semaphore_wait(barrier, 2)
    if EXPLICIT:
        per_mxu = 2 * max(size for _, size in chunks) // TILE // 2
        specs = [pltpu.ACC(q)((targets, TILE), jnp.float32) for q in range(2) for _ in range(per_mxu + 1)]
        pl.run_scoped(body, *specs)
    else:
        body(*[None] * 4)


def solution(mesh):
    group_size = mesh.shape['feat']

    def local_run(x_local, coef_local, targets_local, step_local):
        samples, local_features = x_local.shape
        targets = coef_local.shape[1]
        features = local_features * group_size
        lasso_weight = 0.3 * group_size / features ** 0.5
        chunks = chunk_list(samples)
        count = len(chunks)
        any_spec = pl.BlockSpec(memory_space=pl.ANY)
        vmem_spec = pl.BlockSpec(memory_space=pltpu.VMEM)
        dma = pltpu.SemaphoreType.DMA
        w_t, r_t = pl.pallas_call(
            functools.partial(kernel, chunks, lasso_weight, samples),
            out_shape=(jax.ShapeDtypeStruct((targets, local_features), jnp.float32), jax.ShapeDtypeStruct((targets, samples), jnp.float32)),
            in_specs=[any_spec, vmem_spec, any_spec, vmem_spec],
            out_specs=(vmem_spec, any_spec),
            scratch_shapes=[
                pltpu.VMEM((samples, local_features), jnp.bfloat16),
                pltpu.VMEM((targets, samples), jnp.float32),
                pltpu.VMEM((2, 4, targets, samples), jnp.bfloat16),
                pltpu.VMEM((targets, local_features), jnp.float32),
                pltpu.VMEM((targets, local_features), jnp.float32),
                pltpu.VMEM((targets, local_features), jnp.float32),
                dma((count,)), dma, dma((count,)),
                dma((2, count)), dma((2, count)), dma((2, count)), dma((2, count)), dma((2, count)), dma((2, count)),
            ],
            compiler_params=pltpu.CompilerParams(collective_id=0, has_side_effects=True, vmem_limit_bytes=60 * 1024 * 1024),
            name='block_lasso',
        )(x_local, coef_local.T, targets_local.T, step_local[None, :])
        return w_t.T, r_t.T

    return jax.shard_map(local_run, mesh=mesh, in_specs=(P('prob', 'feat'), P(('prob', 'feat'), None), P('prob', None), P(('prob', 'feat'))), out_specs=(P(('prob', 'feat'), None), P('prob', None)), check_vma=False)
```

time: 358 us -> 88 us (0.25)
  waiting for transfers between devices: 210 us -> 0 us
  matrix products: 127 us -> 0 us
  Pallas kernels: 0 us -> 83.9 us
  between operations: 14.2 us -> 0.64 us
  other arithmetic: 5.3 us -> 0 us
    psum x7 -> x0, waiting for transfers between devices: 210 us -> none  [summed_product(): return lax.psum(product.astype(jnp.bfloat16).astype(jnp.float32), 'feat')]
    dot_general x13 -> x0, matrix products: 127 us -> none  [the longest x7 77 us: summed_product(): jnp.dot(x_local, values.astype(jnp.bfloat16), preferred_element_type=jnp....]
    pallas_call x0 -> x1, Pallas kernels: none -> 83.9 us  [local_run(): pl.pallas_call(functools.partial(kernel, chunks, lasso_weight, samples),...]
    sub x4 -> x0, other arithmetic: 5.29 us -> none  [the longest x3 4.2 us: local_run(): residual = residual - COMBINE_WEIGHT * summed_product(change)]
  transfers between devices with their start and end apart: 7 -> 0, of which waited for: 7 -> 0; matrix products, arithmetic and copies ran while one was open for 0% -> 0% of each run, Pallas kernels for 0% -> 0%
where the time goes in v1:
time: 88 us; the launch traced here: 87.7 us
  Pallas kernels  83.9 us (95%)
  local copies, waits for them, and re-layouts  3.19 us (4%)
    pallas_call x1, Pallas kernels, local_run(): pl.pallas_call(functools.partial(kernel, chunks, lasso_weight, samples),...  83.9 us
    unnamed x2, local copies, waits for them, and re-layouts  3.19 us

profile of v1, /device:TPU:0, one launch (start us, length us, event | category | flops | bytes accessed | tf_op | source)
XLA Modules:
  0.0 87.7 jit_solution(10423581900983461263)
XLA Ops:
  0.6 83.9 %block_lasso.1 = (f32[8,512]{1,0:T(8,128)}, f32[8,16384]{1,0:T(8,128)}) custom-call(bf16[16384,512]{1,0:T(8,128)(2,1)} %refs_0_.1, f32[8,512]{1,0:T(8,128)} %bitcast.8, f32[8,16384]{1,0:T(8,128)} %bitcast.6, f32[1,512]{1,0:T(1,128)} %bitcast.9), custom_call_target="tpu_custom_call" | custom-call | tf_op jit(solution)/shard_map/block_lasso/pallas_call | solution.py:202
  84.5 1.3 %copy.8 = f32[512,8]{0,1:T(8,128)} copy(f32[512,8]{0,1:T(8,128)} %bitcast.7) | data formatting | bytes 32768
  85.8 1.9 %copy.9 = f32[16384,8]{0,1:T(8,128)} copy(f32[16384,8]{0,1:T(8,128)} %bitcast.5) | data formatting | bytes 1048576

commit v2 on v0

v2 whole, which is shorter than its diff:
```python
import functools

import jax
import jax.numpy as jnp
from jax import lax
from jax.experimental import pallas as pl
from jax.experimental.pallas import tpu as pltpu
from jax.sharding import PartitionSpec as P

SWEEPS = 6
COMBINE_WEIGHT = 0.8
LAG = 3
TILE = 256
MESH = pl.DeviceIdType.MESH
OWN, PARTNER, CROSS, RELAYED = 0, 1, 2, 3


def chunk_list(samples):
    size = samples // 16
    return [(i * size, size) for i in range(16)]


def kernel(chunks, lasso_weight, samples, *refs):
    (x_hbm, w0_ref, y_hbm, eta_ref, wv, rv, xv, xt, ubuf, dwv, x_sem, y_sem,
     own_send, cross_send, relay_send, own_recv, cross_recv, relay_recv) = refs
    count = len(chunks)
    targets = w0_ref.shape[0]
    me = lax.axis_index('feat')
    partner = me + 1 - 2 * lax.rem(me, 2)
    cross = 3 - me

    def rows_of(c):
        start, size = chunks[c]
        return pl.ds(start, size)

    def tiles_of(c):
        start, size = chunks[c]
        return range(start // TILE, (start + size) // TILE)

    def x_copy(c):
        return pltpu.make_async_copy(x_hbm.at[rows_of(c)], xv.at[rows_of(c)], x_sem.at[c])

    def remote(par, c, src, dst, peer, send_sem, recv_sem):
        return pltpu.make_async_remote_copy(
            src_ref=ubuf.at[par, src, :, rows_of(c)], dst_ref=ubuf.at[par, dst, :, rows_of(c)],
            send_sem=send_sem.at[par, c], recv_sem=recv_sem.at[par, c], device_id={'feat': peer}, device_id_type=MESH)

    def own_copy(par, c):
        return remote(par, c, OWN, PARTNER, partner, own_send, own_recv)

    def cross_copy(par, c):
        return remote(par, c, OWN, CROSS, cross, cross_send, cross_recv)

    def relay_copy(par, c):
        return remote(par, c, CROSS, RELAYED, partner, relay_send, relay_recv)

    def forward(par, c, first):
        change = dwv[...]
        for t in tiles_of(c):
            rows = pl.ds(t * TILE, TILE)
            if first:
                x_t = xv[rows, :].T
                xt[t] = x_t
            else:
                x_t = xt[t]
            product = jnp.dot(change, x_t, preferred_element_type=jnp.float32)
            ubuf[par, OWN, :, rows] = product.astype(jnp.bfloat16)

    def update_weights(gradient):
        eta = jnp.broadcast_to(eta_ref[...], gradient.shape)
        threshold = eta * lasso_weight
        weights = wv[...]
        stepped = weights + eta * (gradient * (1.0 / samples))
        shrunk = jnp.where(stepped > threshold, stepped - threshold, jnp.where(stepped < -threshold, stepped + threshold, 0.0))
        change = shrunk - weights
        wv[...] = weights + COMBINE_WEIGHT * change
        dwv[...] = change.astype(jnp.bfloat16)

    def wait_sends(par):
        for c in range(count):
            own_copy(par, c).wait_send()
            cross_copy(par, c).wait_send()
            relay_copy(par, c).wait_send()

    def phase(par, first=False, last=False):
        for c in range(count):
            if first:
                x_copy(c).wait()
            forward(par, c, first)
            if c == count // 2 and not first:
                wait_sends(1 - par)
            cross_copy(par, c).start()
            own_copy(par, c).start()
        if first:
            pltpu.make_async_copy(y_hbm, rv, y_sem).wait()
        gradient = None
        for step in range(count + LAG):
            if step < count:
                cross_copy(par, step).wait_recv()
                relay_copy(par, step).start()
            c = step - LAG
            if c < 0:
                continue
            own_copy(par, c).wait_recv()
            relay_copy(par, c).wait_recv()
            rows = rows_of(c)
            u = [ubuf[par, slot, :, rows].astype(jnp.float32) for slot in range(4)]
            total = (u[OWN] + u[PARTNER]) + (u[CROSS] + u[RELAYED])
            residual = rv[:, rows] - (total if first else COMBINE_WEIGHT * total)
            rv[:, rows] = residual
            if not last:
                part = jnp.dot(residual.astype(jnp.bfloat16), xv[rows, :], preferred_element_type=jnp.float32)
                gradient = part if gradient is None else gradient + part
        if not last:
            update_weights(gradient)

    for c in range(count):
        x_copy(c).start()
        if c == 0:
            pltpu.make_async_copy(y_hbm, rv, y_sem).start()
    barrier = pltpu.get_barrier_semaphore()
    for peer in (partner, cross):
        pl.semaphore_signal(barrier, inc=1, device_id={'feat': peer}, device_id_type=MESH)
    wv[...] = w0_ref[...]
    dwv[...] = w0_ref[...].astype(jnp.bfloat16)
    pl.semaphore_wait(barrier, 2)

    phase(0, first=True)

    def sweep(s, carry):
        phase(lax.rem(s, 2))
        return carry

    lax.fori_loop(1, SWEEPS, sweep, 0)
    phase(SWEEPS % 2, last=True)
    wait_sends(SWEEPS % 2)


def solution(mesh):
    group_size = mesh.shape['feat']

    def local_run(x_local, coef_local, targets_local, step_local):
        samples, local_features = x_local.shape
        targets = coef_local.shape[1]
        features = local_features * group_size
        lasso_weight = 0.3 * group_size / features ** 0.5
        chunks = chunk_list(samples)
        count = len(chunks)
        any_spec = pl.BlockSpec(memory_space=pl.ANY)
        vmem_spec = pl.BlockSpec(memory_space=pltpu.VMEM)
        dma = pltpu.SemaphoreType.DMA
        w_t, r_t = pl.pallas_call(
            functools.partial(kernel, chunks, lasso_weight, samples),
            out_shape=(pltpu.VMEM((targets, local_features), jnp.float32), pltpu.VMEM((targets, samples), jnp.float32)),
            in_specs=[pl.BlockSpec(memory_space=pltpu.HBM), vmem_spec, pl.BlockSpec(memory_space=pltpu.HBM), vmem_spec],
            out_specs=(vmem_spec, vmem_spec),
            scratch_shapes=[
                pltpu.VMEM((samples, local_features), jnp.bfloat16),
                pltpu.VMEM((samples // TILE, local_features, TILE), jnp.bfloat16),
                pltpu.VMEM((2, 4, targets, samples), jnp.bfloat16),
                pltpu.VMEM((targets, local_features), jnp.bfloat16),
                dma((count,)), dma,
                dma((2, count)), dma((2, count)), dma((2, count)), dma((2, count)), dma((2, count)), dma((2, count)),
            ],
            compiler_params=pltpu.CompilerParams(collective_id=0, has_side_effects=True, vmem_limit_bytes=60 * 1024 * 1024),
            name='block_lasso',
        )(x_local, coef_local.T, targets_local.T, step_local[None, :])
        return w_t.T, r_t.T

    return jax.shard_map(local_run, mesh=mesh, in_specs=(P('prob', 'feat'), P(('prob', 'feat'), None), P('prob', None), P(('prob', 'feat'))), out_specs=(P(('prob', 'feat'), None), P('prob', None)), check_vma=False)
```

time: 358 us -> 74.4 us (0.21)
  waiting for transfers between devices: 210 us -> 0 us
  matrix products: 127 us -> 0 us
  Pallas kernels: 0 us -> 72.2 us
  between operations: 14.2 us -> 0.64 us
  other arithmetic: 5.3 us -> 0 us
    psum x7 -> x0, waiting for transfers between devices: 210 us -> none  [summed_product(): return lax.psum(product.astype(jnp.bfloat16).astype(jnp.float32), 'feat')]
    dot_general x13 -> x0, matrix products: 127 us -> none  [the longest x7 77 us: summed_product(): jnp.dot(x_local, values.astype(jnp.bfloat16), preferred_element_type=jnp....]
    pallas_call x0 -> x1, Pallas kernels: none -> 72.2 us  [local_run(): pl.pallas_call(functools.partial(kernel, chunks, lasso_weight, samples),...]
    sub x4 -> x0, other arithmetic: 5.29 us -> none  [the longest x3 4.2 us: local_run(): residual = residual - COMBINE_WEIGHT * summed_product(change)]
  transfers between devices with their start and end apart: 7 -> 0, of which waited for: 7 -> 0; matrix products, arithmetic and copies ran while one was open for 0% -> 0% of each run, Pallas kernels for 0% -> 0%
where the time goes in v2:
time: 74.4 us; the launch traced here: 74.2 us
  Pallas kernels  72.2 us (97%)
  local copies, waits for them, and re-layouts  1.4 us (2%)
    pallas_call x1, Pallas kernels, local_run(): pl.pallas_call(functools.partial(kernel, chunks, lasso_weight, samples),...  72.2 us

profile of v2, /device:TPU:0, one launch (start us, length us, event | category | flops | bytes accessed | tf_op | source)
XLA Modules:
  0.0 74.2 jit_solution(5026652133051351225)
XLA Ops:
  0.6 72.2 %block_lasso.1 = (f32[8,512]{1,0:T(8,128)S(1)}, f32[8,16384]{1,0:T(8,128)S(1)}) custom-call(bf16[16384,512]{1,0:T(8,128)(2,1)} %refs_0_.1, f32[8,512]{1,0:T(8,128)} %bitcast.8, f32[8,16384]{1,0:T(8,128)} %bitcast.7, f32[1,512]{1,0:T(1,128)} %bitcast.9), custom_call_target="tpu_custom_call" | custom-call | tf_op jit(solution)/shard_map/block_lasso/pallas_call | solution.py:152
  72.8 0.6 copy.8
  73.4 0.8 %copy.9 = f32[16384,8]{0,1:T(8,128)} copy(f32[16384,8]{0,1:T(8,128)S(1)} %bitcast.5) | data formatting | bytes 1048576

commit v3 on v2

--- a/solution.py
+++ b/solution.py
@@ -27,7 +27,7 @@
     targets = w0_ref.shape[0]
     me = lax.axis_index('feat')
     partner = me + 1 - 2 * lax.rem(me, 2)
-    cross = 3 - me
+    cross = lax.rem(me + 2, 4)
 
     def rows_of(c):
         start, size = chunks[c]

time: 74.4 us -> 75.4 us (1.013)
  Pallas kernels: 72.2 us -> 73.1 us
    pallas_call x1, Pallas kernels: 72.2 us -> 73.1 us  [local_run(): pl.pallas_call(functools.partial(kernel, chunks, lasso_weight, samples),...]
where the time goes in v3:
time: 75.4 us; the launch traced here: 75.2 us
  Pallas kernels  73.1 us (97%)
  local copies, waits for them, and re-layouts  1.4 us (2%)
    pallas_call x1, Pallas kernels, local_run(): pl.pallas_call(functools.partial(kernel, chunks, lasso_weight, samples),...  73.1 us

profile of v3, /device:TPU:0, one launch (start us, length us, event | category | flops | bytes accessed | tf_op | source)
XLA Modules:
  0.0 75.2 jit_solution(13107948100180248333)
XLA Ops:
  0.6 73.1 %block_lasso.1 = (f32[8,512]{1,0:T(8,128)S(1)}, f32[8,16384]{1,0:T(8,128)S(1)}) custom-call(bf16[16384,512]{1,0:T(8,128)(2,1)} %refs_0_.1, f32[8,512]{1,0:T(8,128)} %bitcast.8, f32[8,16384]{1,0:T(8,128)} %bitcast.7, f32[1,512]{1,0:T(1,128)} %bitcast.9), custom_call_target="tpu_custom_call" | custom-call | tf_op jit(solution)/shard_map/block_lasso/pallas_call | solution.py:152
  73.8 0.6 copy.8
  74.4 0.8 %copy.9 = f32[16384,8]{0,1:T(8,128)} copy(f32[16384,8]{0,1:T(8,128)S(1)} %bitcast.5) | data formatting | bytes 1048576

commit v4 on v2

v4 whole, which is shorter than its diff:
```python
import functools

import jax
import jax.numpy as jnp
from jax import lax
from jax.experimental import pallas as pl
from jax.experimental.pallas import tpu as pltpu
from jax.sharding import PartitionSpec as P

SWEEPS = 6
COMBINE_WEIGHT = 0.8
TILE = 256
MESH = pl.DeviceIdType.MESH
OWN, PARTNER, CROSS, DIAGONAL = 0, 1, 2, 3
PIECE = 512
GROUPS = 6
CHUNK = 1024
TWICE = 0


def kernel(samples, lasso_weight, *refs):
    (x_hbm, w0_ref, y_hbm, eta_ref, wv, rv, xv, xt, ubuf, rbuf, dwv, x_sem, y_sem,
     u_own_send, u_cross_send, u_diag_send, u_own_recv, u_cross_recv, u_diag_recv,
     r_own_send, r_cross_send, r_diag_send, r_own_recv, r_cross_recv, r_diag_recv) = refs
    me = lax.axis_index('feat')
    partner = me + 1 - 2 * lax.rem(me, 2)
    cross = 3 - me
    diagonal = lax.rem(me + 2, 4)
    owned_rows = GROUPS * 4 * PIECE
    units = GROUPS + (samples - owned_rows) // CHUNK
    groups = range(GROUPS)
    shared = range(GROUPS, units)

    def start_of(g, who):
        return g * 4 * PIECE + who * PIECE

    def piece(g, who):
        return pl.ds(pl.multiple_of(start_of(g, who), PIECE), PIECE)

    def chunk(d):
        return pl.ds(owned_rows + (d - GROUPS) * CHUNK, CHUNK)

    def x_copy(unit, who):
        rows = chunk(unit) if who is None else piece(unit, who)
        index = 0 if who is None else who
        return pltpu.make_async_copy(x_hbm.at[rows], xv.at[rows], x_sem.at[unit, index])

    def u_copy(par, unit, rows, src, dst, peer, sems):
        send_sem, recv_sem = sems
        return pltpu.make_async_remote_copy(
            src_ref=ubuf.at[par, src, :, rows], dst_ref=ubuf.at[par, dst, :, rows],
            send_sem=send_sem.at[par, unit], recv_sem=recv_sem.at[par, unit], device_id={'feat': peer}, device_id_type=MESH)

    def r_copy(par, last, g, who, peer, sems):
        send_sem, recv_sem = sems
        rows = piece(g, who)
        ref = rv.at[:, rows] if last else rbuf.at[par, :, rows]
        return pltpu.make_async_remote_copy(
            src_ref=ref, dst_ref=ref, send_sem=send_sem.at[par, g], recv_sem=recv_sem.at[par, g], device_id={'feat': peer}, device_id_type=MESH)

    own_sems, cross_sems, diag_sems = (u_own_send, u_own_recv), (u_cross_send, u_cross_recv), (u_diag_send, u_diag_recv)
    r_own_sems, r_cross_sems, r_diag_sems = (r_own_send, r_own_recv), (r_cross_send, r_cross_recv), (r_diag_send, r_diag_recv)

    def group_copies(par, g, receive=False):
        rows = [piece(g, me)] * 3 if receive else [piece(g, cross), piece(g, diagonal), piece(g, partner)]
        return [u_copy(par, g, rows[0], OWN, CROSS, cross, cross_sems), u_copy(par, g, rows[1], OWN, DIAGONAL, diagonal, diag_sems), u_copy(par, g, rows[2], OWN, PARTNER, partner, own_sems)]

    def chunk_copies(par, d):
        rows = chunk(d)
        return [u_copy(par, d, rows, OWN, CROSS, cross, cross_sems), u_copy(par, d, rows, OWN, PARTNER, partner, own_sems), u_copy(par, d, rows, CROSS, DIAGONAL, partner, diag_sems)]

    def r_twice(g):
        return g >= GROUPS - TWICE

    def return_copies(par, last, g):
        return [r_copy(par, last, g, me, cross, r_cross_sems), r_copy(par, last, g, me, partner, r_own_sems),
                r_copy(par, last, g, me, diagonal, r_diag_sems) if r_twice(g) else r_copy(par, last, g, cross, partner, r_diag_sems)]

    def forward(par, start, size, first):
        change = dwv[...]
        for i in range(size // TILE):
            rows = pl.ds(start + i * TILE if isinstance(start, int) else pl.multiple_of(start + i * TILE, TILE), TILE)
            t = start // TILE + i
            if first:
                x_t = xv[rows, :].T
                xt[t] = x_t
            else:
                x_t = xt[t]
            product = jnp.dot(change, x_t, preferred_element_type=jnp.float32)
            ubuf[par, OWN, :, rows] = product.astype(jnp.bfloat16)

    def new_residual(par, rows, first):
        u = [ubuf[par, slot, :, rows].astype(jnp.float32) for slot in range(4)]
        total = (u[OWN] + u[PARTNER]) + (u[CROSS] + u[DIAGONAL])
        residual = rv[:, rows] - (total if first else COMBINE_WEIGHT * total)
        rv[:, rows] = residual
        return residual

    def update_weights(gradient):
        eta = jnp.broadcast_to(eta_ref[...], gradient.shape)
        threshold = eta * lasso_weight
        weights = wv[...]
        stepped = weights + eta * (gradient * (1.0 / samples))
        shrunk = jnp.where(stepped > threshold, stepped - threshold, jnp.where(stepped < -threshold, stepped + threshold, 0.0))
        change = shrunk - weights
        wv[...] = weights + COMBINE_WEIGHT * change
        dwv[...] = change.astype(jnp.bfloat16)

    def wait_sends(par, last=False):
        for g in groups:
            for copy in group_copies(par, g) + return_copies(par, last, g):
                copy.wait_send()
        for d in shared:
            for copy in chunk_copies(par, d):
                copy.wait_send()

    def phase(par, first=False, last=False):
        parts = []

        def add_gradient(lhs, rows):
            part = jnp.dot(lhs, xv[rows, :], preferred_element_type=jnp.float32)
            parts[:] = [part if not parts else parts[0] + part]

        for g in groups:
            for i, who in enumerate((cross, diagonal, partner, me)):
                if first:
                    x_copy(g, who).wait()
                forward(par, start_of(g, who), PIECE, first)
                if i < 3:
                    group_copies(par, g)[i].start()
        for d in shared:
            if first:
                x_copy(d, None).wait()
            forward(par, owned_rows + (d - GROUPS) * CHUNK, CHUNK, first)
            if d == units - 1 and not first:
                wait_sends(1 - par)
            to_cross, to_partner, _ = chunk_copies(par, d)
            to_cross.start()
            to_partner.start()
        if first:
            pltpu.make_async_copy(y_hbm, rv, y_sem).wait()

        def owner_step(g):
            for copy in group_copies(par, g, receive=True):
                copy.wait_recv()
            rows = piece(g, me)
            residual = new_residual(par, rows, first)
            if not last:
                rounded = residual.astype(jnp.bfloat16)
                rbuf[par, :, rows] = rounded
            to_cross, to_partner, third = return_copies(par, last, g)
            to_cross.start()
            if r_twice(g):
                third.start()
            to_partner.start()
            if not last:
                add_gradient(rounded, rows)

        def take(g, who):
            if not last:
                add_gradient(rbuf[par, :, piece(g, who)], piece(g, who))

        def partner_step(g):
            r_copy(par, last, g, partner, partner, r_own_sems).wait_recv()
            take(g, partner)

        def cross_step(g):
            r_copy(par, last, g, cross, cross, r_cross_sems).wait_recv()
            if not r_twice(g):
                return_copies(par, last, g)[2].start()
            take(g, cross)

        def diagonal_step(g):
            r_copy(par, last, g, diagonal, partner, r_diag_sems).wait_recv()
            take(g, diagonal)

        def relay_step(d):
            to_cross, _, relay = chunk_copies(par, d)
            to_cross.wait_recv()
            relay.start()

        def shared_step(d):
            _, to_partner, relay = chunk_copies(par, d)
            to_partner.wait_recv()
            relay.wait_recv()
            residual = new_residual(par, chunk(d), first)
            if not last:
                add_gradient(residual.astype(jnp.bfloat16), chunk(d))

        for g in groups:
            owner_step(g)
        for d in shared:
            relay_step(d)
        for g in groups:
            partner_step(g)
        waiting = list(shared)
        for g in groups:
            if waiting and g % 2 == 0:
                shared_step(waiting.pop(0))
            cross_step(g)
        for d in waiting:
            shared_step(d)
        for g in groups:
            diagonal_step(g)
        if not last:
            update_weights(parts[0])

    for g in groups:
        for who in (cross, diagonal, partner, me):
            x_copy(g, who).start()
        if g == 0:
            pltpu.make_async_copy(y_hbm, rv, y_sem).start()
    for d in shared:
        x_copy(d, None).start()
    barrier = pltpu.get_barrier_semaphore()
    for peer in (partner, cross, diagonal):
        pl.semaphore_signal(barrier, inc=1, device_id={'feat': peer}, device_id_type=MESH)
    wv[...] = w0_ref[...]
    dwv[...] = w0_ref[...].astype(jnp.bfloat16)
    pl.semaphore_wait(barrier, 3)

    phase(0, first=True)

    def sweep(s, carry):
        phase(lax.rem(s, 2))
        return carry

    lax.fori_loop(1, SWEEPS, sweep, 0)
    phase(SWEEPS % 2, last=True)
    wait_sends(SWEEPS % 2, last=True)


def solution(mesh):
    group_size = mesh.shape['feat']

    def local_run(x_local, coef_local, targets_local, step_local):
        samples, local_features = x_local.shape
        targets = coef_local.shape[1]
        features = local_features * group_size
        lasso_weight = 0.3 * group_size / features ** 0.5
        units = GROUPS + (samples - GROUPS * 4 * PIECE) // CHUNK
        hbm_spec = pl.BlockSpec(memory_space=pltpu.HBM)
        vmem_spec = pl.BlockSpec(memory_space=pltpu.VMEM)
        dma = pltpu.SemaphoreType.DMA
        w_t, r_t = pl.pallas_call(
            functools.partial(kernel, samples, lasso_weight),
            out_shape=(pltpu.VMEM((targets, local_features), jnp.float32), pltpu.VMEM((targets, samples), jnp.float32)),
            in_specs=[hbm_spec, vmem_spec, hbm_spec, vmem_spec],
            out_specs=(vmem_spec, vmem_spec),
            scratch_shapes=[
                pltpu.VMEM((samples, local_features), jnp.bfloat16),
                pltpu.VMEM((samples // TILE, local_features, TILE), jnp.bfloat16),
                pltpu.VMEM((2, 4, targets, samples), jnp.bfloat16),
                pltpu.VMEM((2, targets, samples), jnp.bfloat16),
                pltpu.VMEM((targets, local_features), jnp.bfloat16),
                dma((units, 4)), dma,
                *[dma((2, units))] * 6, *[dma((2, GROUPS))] * 6,
            ],
            compiler_params=pltpu.CompilerParams(collective_id=0, has_side_effects=True, vmem_limit_bytes=60 * 1024 * 1024),
            name='block_lasso',
        )(x_local, coef_local.T, targets_local.T, step_local[None, :])
        return w_t.T, r_t.T

    return jax.shard_map(local_run, mesh=mesh, in_specs=(P('prob', 'feat'), P(('prob', 'feat'), None), P('prob', None), P(('prob', 'feat'))), out_specs=(P(('prob', 'feat'), None), P('prob', None)), check_vma=False)
```

time: 74.4 us -> 82.7 us (1.11)
  Pallas kernels: 72.2 us -> 80.4 us
    pallas_call x1, Pallas kernels: 72.2 us -> 80.4 us  [local_run(): pl.pallas_call(functools.partial(kernel, samples, lasso_weight), out_shap...]
where the time goes in v4:
time: 82.7 us; the launch traced here: 82.5 us
  Pallas kernels  80.4 us (97%)
  local copies, waits for them, and re-layouts  1.4 us (2%)
    pallas_call x1, Pallas kernels, local_run(): pl.pallas_call(functools.partial(kernel, samples, lasso_weight), out_shap...  80.4 us

profile of v4, /device:TPU:0, one launch (start us, length us, event | category | flops | bytes accessed | tf_op | source)
XLA Modules:
  0.0 82.5 jit_solution(7628754896039961951)
XLA Ops:
  0.6 80.4 %block_lasso.1 = (f32[8,512]{1,0:T(8,128)S(1)}, f32[8,16384]{1,0:T(8,128)S(1)}) custom-call(bf16[16384,512]{1,0:T(8,128)(2,1)} %refs_0_.1, f32[8,512]{1,0:T(8,128)} %bitcast.8, f32[8,16384]{1,0:T(8,128)} %bitcast.7, f32[1,512]{1,0:T(1,128)} %bitcast.9), custom_call_target="tpu_custom_call" | custom-call | tf_op jit(solution)/shard_map/block_lasso/pallas_call | solution.py:245
  81.1 0.6 copy.8
  81.7 0.8 copy.9

commit v5 on v2

--- a/solution.py
+++ b/solution.py
@@ -10,14 +10,15 @@
 SWEEPS = 6
 COMBINE_WEIGHT = 0.8
 LAG = 3
+TWICE = 1
 TILE = 256
 MESH = pl.DeviceIdType.MESH
 OWN, PARTNER, CROSS, RELAYED = 0, 1, 2, 3
 
 
 def chunk_list(samples):
-    size = samples // 16
-    return [(i * size, size) for i in range(16)]
+    sizes = [512, 512] + [1024] * ((samples - 2048) // 1024) + [512, 512]
+    return [(sum(sizes[:i]), size) for i, size in enumerate(sizes)]
 
 
 def kernel(chunks, lasso_weight, samples, *refs):
@@ -28,6 +29,7 @@
     me = lax.axis_index('feat')
     partner = me + 1 - 2 * lax.rem(me, 2)
     cross = 3 - me
+    diagonal = lax.rem(me + 2, 4)
 
     def rows_of(c):
         start, size = chunks[c]
@@ -51,7 +53,12 @@
     def cross_copy(par, c):
         return remote(par, c, OWN, CROSS, cross, cross_send, cross_recv)
 
+    def twice(c):
+        return c >= count - TWICE
+
     def relay_copy(par, c):
+        if twice(c):
+            return remote(par, c, OWN, RELAYED, diagonal, relay_send, relay_recv)
         return remote(par, c, CROSS, RELAYED, partner, relay_send, relay_recv)
 
     def forward(par, c, first):
@@ -89,6 +96,8 @@
             forward(par, c, first)
             if c == count // 2 and not first:
                 wait_sends(1 - par)
+            if twice(c):
+                relay_copy(par, c).start()
             cross_copy(par, c).start()
             own_copy(par, c).start()
         if first:
@@ -97,7 +106,8 @@
         for step in range(count + LAG):
             if step < count:
                 cross_copy(par, step).wait_recv()
-                relay_copy(par, step).start()
+                if not twice(step):
+                    relay_copy(par, step).start()
             c = step - LAG
             if c < 0:
                 continue
@@ -119,11 +129,11 @@
         if c == 0:
             pltpu.make_async_copy(y_hbm, rv, y_sem).start()
     barrier = pltpu.get_barrier_semaphore()
-    for peer in (partner, cross):
+    for peer in (partner, cross, diagonal):
         pl.semaphore_signal(barrier, inc=1, device_id={'feat': peer}, device_id_type=MESH)
     wv[...] = w0_ref[...]
     dwv[...] = w0_ref[...].astype(jnp.bfloat16)
-    pl.semaphore_wait(barrier, 2)
+    pl.semaphore_wait(barrier, 3)
 
     phase(0, first=True)
 

time: 74.4 us -> 78.7 us (1.058)
  Pallas kernels: 72.2 us -> 76.5 us
    pallas_call x1, Pallas kernels: 72.2 us -> 76.5 us  [local_run(): pl.pallas_call(functools.partial(kernel, chunks, lasso_weight, samples),...]
where the time goes in v5:
time: 78.7 us; the launch traced here: 78.5 us
  Pallas kernels  76.5 us (97%)
  local copies, waits for them, and re-layouts  1.4 us (2%)
    pallas_call x1, Pallas kernels, local_run(): pl.pallas_call(functools.partial(kernel, chunks, lasso_weight, samples),...  76.5 us

profile of v5, /device:TPU:0, one launch (start us, length us, event | category | flops | bytes accessed | tf_op | source)
XLA Modules:
  0.0 78.5 jit_solution(7130570132423665512)
XLA Ops:
  0.6 76.5 %block_lasso.1 = (f32[8,512]{1,0:T(8,128)S(1)}, f32[8,16384]{1,0:T(8,128)S(1)}) custom-call(bf16[16384,512]{1,0:T(8,128)(2,1)} %refs_0_.1, f32[8,512]{1,0:T(8,128)} %bitcast.8, f32[8,16384]{1,0:T(8,128)} %bitcast.7, f32[1,512]{1,0:T(1,128)} %bitcast.9), custom_call_target="tpu_custom_call" | custom-call | tf_op jit(solution)/shard_map/block_lasso/pallas_call | solution.py:162
  77.1 0.6 copy.8
  77.7 0.8 %copy.9 = f32[16384,8]{0,1:T(8,128)} copy(f32[16384,8]{0,1:T(8,128)S(1)} %bitcast.5) | data formatting | bytes 1048576

commit v6 on v2

--- a/solution.py
+++ b/solution.py
@@ -9,15 +9,15 @@
 
 SWEEPS = 6
 COMBINE_WEIGHT = 0.8
-LAG = 3
+LAG = 2
 TILE = 256
 MESH = pl.DeviceIdType.MESH
 OWN, PARTNER, CROSS, RELAYED = 0, 1, 2, 3
 
 
 def chunk_list(samples):
-    size = samples // 16
-    return [(i * size, size) for i in range(16)]
+    size = samples // 8
+    return [(i * size, size) for i in range(8)]
 
 
 def kernel(chunks, lasso_weight, samples, *refs):

time: 74.4 us -> 71.1 us (0.956)
  Pallas kernels: 72.2 us -> 68.9 us
    pallas_call x1, Pallas kernels: 72.2 us -> 68.9 us  [local_run(): pl.pallas_call(functools.partial(kernel, chunks, lasso_weight, samples),...]
where the time goes in v6:
time: 71.1 us; the launch traced here: 70.9 us
  Pallas kernels  68.9 us (97%)
  local copies, waits for them, and re-layouts  1.4 us (2%)
    pallas_call x1, Pallas kernels, local_run(): pl.pallas_call(functools.partial(kernel, chunks, lasso_weight, samples),...  68.9 us

profile of v6, /device:TPU:0, one launch (start us, length us, event | category | flops | bytes accessed | tf_op | source)
XLA Modules:
  0.0 70.9 jit_solution(1045842079488091503)
XLA Ops:
  0.6 68.9 %block_lasso.1 = (f32[8,512]{1,0:T(8,128)S(1)}, f32[8,16384]{1,0:T(8,128)S(1)}) custom-call(bf16[16384,512]{1,0:T(8,128)(2,1)} %refs_0_.1, f32[8,512]{1,0:T(8,128)} %bitcast.8, f32[8,16384]{1,0:T(8,128)} %bitcast.7, f32[1,512]{1,0:T(1,128)} %bitcast.9), custom_call_target="tpu_custom_call" | custom-call | tf_op jit(solution)/shard_map/block_lasso/pallas_call | solution.py:152
  69.5 0.6 copy.8
  70.1 0.8 %copy.9 = f32[16384,8]{0,1:T(8,128)} copy(f32[16384,8]{0,1:T(8,128)S(1)} %bitcast.5) | data formatting | bytes 1048576

commit v7 on v6

--- a/solution.py
+++ b/solution.py
@@ -16,12 +16,12 @@
 
 
 def chunk_list(samples):
-    size = samples // 8
-    return [(i * size, size) for i in range(8)]
+    sizes = [512, 1536] + [2048] * (samples // 2048 - 2) + [1024, 1024]
+    return [(sum(sizes[:i]), size) for i, size in enumerate(sizes)]
 
 
 def kernel(chunks, lasso_weight, samples, *refs):
-    (x_hbm, w0_ref, y_hbm, eta_ref, wv, rv, xv, xt, ubuf, dwv, x_sem, y_sem,
+    (x_hbm, w0_ref, y_hbm, eta_ref, wv, rv, xv, xt, ubuf, rbuf, dwv, x_sem, y_sem,
      own_send, cross_send, relay_send, own_recv, cross_recv, relay_recv) = refs
     count = len(chunks)
     targets = w0_ref.shape[0]
@@ -30,6 +30,8 @@
     cross = 3 - me
 
     def rows_of(c):
+        if c is None:
+            return pl.ds(0, samples)
         start, size = chunks[c]
         return pl.ds(start, size)
 
@@ -43,7 +45,7 @@
     def remote(par, c, src, dst, peer, send_sem, recv_sem):
         return pltpu.make_async_remote_copy(
             src_ref=ubuf.at[par, src, :, rows_of(c)], dst_ref=ubuf.at[par, dst, :, rows_of(c)],
-            send_sem=send_sem.at[par, c], recv_sem=recv_sem.at[par, c], device_id={'feat': peer}, device_id_type=MESH)
+            send_sem=send_sem.at[par], recv_sem=recv_sem.at[par] if c is None or src == dst - 1 == OWN else recv_sem.at[par, c], device_id={'feat': peer}, device_id_type=MESH)
 
     def own_copy(par, c):
         return remote(par, c, OWN, PARTNER, partner, own_send, own_recv)
@@ -77,10 +79,9 @@
         dwv[...] = change.astype(jnp.bfloat16)
 
     def wait_sends(par):
-        for c in range(count):
-            own_copy(par, c).wait_send()
-            cross_copy(par, c).wait_send()
-            relay_copy(par, c).wait_send()
+        own_copy(par, None).wait_send()
+        cross_copy(par, None).wait_send()
+        relay_copy(par, None).wait_send()
 
     def phase(par, first=False, last=False):
         for c in range(count):
@@ -94,22 +95,24 @@
         if first:
             pltpu.make_async_copy(y_hbm, rv, y_sem).wait()
         gradient = None
-        for step in range(count + LAG):
+        for step in range(count + LAG + 1):
             if step < count:
                 cross_copy(par, step).wait_recv()
                 relay_copy(par, step).start()
             c = step - LAG
-            if c < 0:
-                continue
-            own_copy(par, c).wait_recv()
-            relay_copy(par, c).wait_recv()
-            rows = rows_of(c)
-            u = [ubuf[par, slot, :, rows].astype(jnp.float32) for slot in range(4)]
-            total = (u[OWN] + u[PARTNER]) + (u[CROSS] + u[RELAYED])
-            residual = rv[:, rows] - (total if first else COMBINE_WEIGHT * total)
-            rv[:, rows] = residual
-            if not last:
-                part = jnp.dot(residual.astype(jnp.bfloat16), xv[rows, :], preferred_element_type=jnp.float32)
+            if c == 0:
+                own_copy(par, None).wait_recv()
+            if 0 <= c < count:
+                relay_copy(par, c).wait_recv()
+                rows = rows_of(c)
+                u = [ubuf[par, slot, :, rows].astype(jnp.float32) for slot in range(4)]
+                total = (u[OWN] + u[PARTNER]) + (u[CROSS] + u[RELAYED])
+                residual = rv[:, rows] - (total if first else COMBINE_WEIGHT * total)
+                rv[:, rows] = residual
+                rbuf[:, rows] = residual.astype(jnp.bfloat16)
+            if c >= 1 and not last:
+                rows = rows_of(c - 1)
+                part = jnp.dot(rbuf[:, rows], xv[rows, :], preferred_element_type=jnp.float32)
                 gradient = part if gradient is None else gradient + part
         if not last:
             update_weights(gradient)
@@ -158,9 +161,10 @@
                 pltpu.VMEM((samples, local_features), jnp.bfloat16),
                 pltpu.VMEM((samples // TILE, local_features, TILE), jnp.bfloat16),
                 pltpu.VMEM((2, 4, targets, samples), jnp.bfloat16),
+                pltpu.VMEM((targets, samples), jnp.bfloat16),
                 pltpu.VMEM((targets, local_features), jnp.bfloat16),
                 dma((count,)), dma,
-                dma((2, count)), dma((2, count)), dma((2, count)), dma((2, count)), dma((2, count)), dma((2, count)),
+                dma((2,)), dma((2,)), dma((2,)), dma((2,)), dma((2, count)), dma((2, count)),
             ],
             compiler_params=pltpu.CompilerParams(collective_id=0, has_side_effects=True, vmem_limit_bytes=60 * 1024 * 1024),
             name='block_lasso',

time: 71.1 us -> 73.8 us (1.038)
  Pallas kernels: 68.9 us -> 71.5 us
    pallas_call x1, Pallas kernels: 68.9 us -> 71.5 us  [local_run(): pl.pallas_call(functools.partial(kernel, chunks, lasso_weight, samples),...]
where the time goes in v7:
time: 73.8 us; the launch traced here: 73.5 us
  Pallas kernels  71.5 us (97%)
  local copies, waits for them, and re-layouts  1.4 us (2%)
    pallas_call x1, Pallas kernels, local_run(): pl.pallas_call(functools.partial(kernel, chunks, lasso_weight, samples),...  71.5 us

profile of v7, /device:TPU:0, one launch (start us, length us, event | category | flops | bytes accessed | tf_op | source)
XLA Modules:
  0.0 73.5 jit_solution(1005898063065095441)
XLA Ops:
  0.6 71.5 %block_lasso.1 = (f32[8,512]{1,0:T(8,128)S(1)}, f32[8,16384]{1,0:T(8,128)S(1)}) custom-call(bf16[16384,512]{1,0:T(8,128)(2,1)} %refs_0_.1, f32[8,512]{1,0:T(8,128)} %bitcast.8, f32[8,16384]{1,0:T(8,128)} %bitcast.7, f32[1,512]{1,0:T(1,128)} %bitcast.9), custom_call_target="tpu_custom_call" | custom-call | tf_op jit(solution)/shard_map/block_lasso/pallas_call | solution.py:155
  72.1 0.6 copy.8
  72.7 0.8 %copy.9 = f32[16384,8]{0,1:T(8,128)} copy(f32[16384,8]{0,1:T(8,128)S(1)} %bitcast.5) | data formatting | bytes 1048576

commit v8 on v7

--- a/solution.py
+++ b/solution.py
@@ -10,6 +10,7 @@
 SWEEPS = 6
 COMBINE_WEIGHT = 0.8
 LAG = 2
+LATE = (1, 3, 5, 7)
 TILE = 256
 MESH = pl.DeviceIdType.MESH
 OWN, PARTNER, CROSS, RELAYED = 0, 1, 2, 3
@@ -56,17 +57,21 @@
     def relay_copy(par, c):
         return remote(par, c, CROSS, RELAYED, partner, relay_send, relay_recv)
 
+    def transpose_x(c):
+        for t in tiles_of(c):
+            xt[t] = xv[pl.ds(t * TILE, TILE), :].T
+
     def forward(par, c, first):
         change = dwv[...]
         for t in tiles_of(c):
             rows = pl.ds(t * TILE, TILE)
             if first:
-                x_t = xv[rows, :].T
-                xt[t] = x_t
+                product = lax.dot_general(change, xv[rows, :], (((1,), (1,)), ((), ())), preferred_element_type=jnp.float32)
             else:
-                x_t = xt[t]
-            product = jnp.dot(change, x_t, preferred_element_type=jnp.float32)
+                product = jnp.dot(change, xt[t], preferred_element_type=jnp.float32)
             ubuf[par, OWN, :, rows] = product.astype(jnp.bfloat16)
+        if first and c not in LATE:
+            transpose_x(c)
 
     def update_weights(gradient):
         eta = jnp.broadcast_to(eta_ref[...], gradient.shape)
@@ -90,6 +95,8 @@
             forward(par, c, first)
             if c == count // 2 and not first:
                 wait_sends(1 - par)
+            if first and c == 0:
+                pl.semaphore_wait(barrier, 2)
             cross_copy(par, c).start()
             own_copy(par, c).start()
         if first:
@@ -99,6 +106,8 @@
             if step < count:
                 cross_copy(par, step).wait_recv()
                 relay_copy(par, step).start()
+            if first and step in LATE:
+                transpose_x(step)
             c = step - LAG
             if c == 0:
                 own_copy(par, None).wait_recv()
@@ -126,8 +135,6 @@
         pl.semaphore_signal(barrier, inc=1, device_id={'feat': peer}, device_id_type=MESH)
     wv[...] = w0_ref[...]
     dwv[...] = w0_ref[...].astype(jnp.bfloat16)
-    pl.semaphore_wait(barrier, 2)
-
     phase(0, first=True)
 
     def sweep(s, carry):

time: 73.8 us -> 74.1 us (level)
  no operation moved by 1% of the time
where the time goes in v8:
time: 74.1 us; the launch traced here: 73.9 us
  Pallas kernels  71.9 us (97%)
  local copies, waits for them, and re-layouts  1.4 us (2%)
    pallas_call x1, Pallas kernels, local_run(): pl.pallas_call(functools.partial(kernel, chunks, lasso_weight, samples),...  71.9 us

profile of v8, /device:TPU:0, one launch (start us, length us, event | category | flops | bytes accessed | tf_op | source)
XLA Modules:
  0.0 73.9 jit_solution(14888627631623700347)
XLA Ops:
  0.6 71.9 %block_lasso.1 = (f32[8,512]{1,0:T(8,128)S(1)}, f32[8,16384]{1,0:T(8,128)S(1)}) custom-call(bf16[16384,512]{1,0:T(8,128)(2,1)} %refs_0_.1, f32[8,512]{1,0:T(8,128)} %bitcast.8, f32[8,16384]{1,0:T(8,128)} %bitcast.7, f32[1,512]{1,0:T(1,128)} %bitcast.9), custom_call_target="tpu_custom_call" | custom-call | tf_op jit(solution)/shard_map/block_lasso/pallas_call | solution.py:162
  72.5 0.6 copy.8
  73.1 0.8 %copy.9 = f32[16384,8]{0,1:T(8,128)} copy(f32[16384,8]{0,1:T(8,128)S(1)} %bitcast.5) | data formatting | bytes 1048576

commit v9 on v8

--- a/solution.py
+++ b/solution.py
@@ -9,30 +9,27 @@
 
 SWEEPS = 6
 COMBINE_WEIGHT = 0.8
-LAG = 2
-LATE = (1, 3, 5, 7)
+RELAY_ROWS = 3072
 TILE = 256
 MESH = pl.DeviceIdType.MESH
 OWN, PARTNER, CROSS, RELAYED = 0, 1, 2, 3
 
 
 def chunk_list(samples):
-    sizes = [512, 1536] + [2048] * (samples // 2048 - 2) + [1024, 1024]
+    sizes = [1024] + [2048] * (samples // 2048 - 1) + [1024]
     return [(sum(sizes[:i]), size) for i, size in enumerate(sizes)]
 
 
 def kernel(chunks, lasso_weight, samples, *refs):
-    (x_hbm, w0_ref, y_hbm, eta_ref, wv, rv, xv, xt, ubuf, rbuf, dwv, x_sem, y_sem,
+    (x_hbm, w0_hbm, y_hbm, eta_hbm, wv, rv, xv, xt, ubuf, dwv, eta_ref, x_sem, small_sem,
      own_send, cross_send, relay_send, own_recv, cross_recv, relay_recv) = refs
     count = len(chunks)
-    targets = w0_ref.shape[0]
+    late = [c for c in range(count) if c % 2 == 1]
     me = lax.axis_index('feat')
     partner = me + 1 - 2 * lax.rem(me, 2)
     cross = 3 - me
 
     def rows_of(c):
-        if c is None:
-            return pl.ds(0, samples)
         start, size = chunks[c]
         return pl.ds(start, size)
 
@@ -43,10 +40,19 @@
     def x_copy(c):
         return pltpu.make_async_copy(x_hbm.at[rows_of(c)], xv.at[rows_of(c)], x_sem.at[c])
 
+    def w_copy():
+        return pltpu.make_async_copy(w0_hbm, wv, small_sem.at[0])
+
+    def y_copy():
+        return pltpu.make_async_copy(y_hbm, rv, small_sem.at[1])
+
+    def eta_copy():
+        return pltpu.make_async_copy(eta_hbm, eta_ref, small_sem.at[2])
+
     def remote(par, c, src, dst, peer, send_sem, recv_sem):
         return pltpu.make_async_remote_copy(
             src_ref=ubuf.at[par, src, :, rows_of(c)], dst_ref=ubuf.at[par, dst, :, rows_of(c)],
-            send_sem=send_sem.at[par], recv_sem=recv_sem.at[par] if c is None or src == dst - 1 == OWN else recv_sem.at[par, c], device_id={'feat': peer}, device_id_type=MESH)
+            send_sem=send_sem.at[par, c], recv_sem=recv_sem.at[par, c], device_id={'feat': peer}, device_id_type=MESH)
 
     def own_copy(par, c):
         return remote(par, c, OWN, PARTNER, partner, own_send, own_recv)
@@ -70,7 +76,7 @@
             else:
                 product = jnp.dot(change, xt[t], preferred_element_type=jnp.float32)
             ubuf[par, OWN, :, rows] = product.astype(jnp.bfloat16)
-        if first and c not in LATE:
+        if first and c not in late:
             transpose_x(c)
 
     def update_weights(gradient):
@@ -84,9 +90,10 @@
         dwv[...] = change.astype(jnp.bfloat16)
 
     def wait_sends(par):
-        own_copy(par, None).wait_send()
-        cross_copy(par, None).wait_send()
-        relay_copy(par, None).wait_send()
+        for c in range(count):
+            own_copy(par, c).wait_send()
+            cross_copy(par, c).wait_send()
+            relay_copy(par, c).wait_send()
 
     def phase(par, first=False, last=False):
         for c in range(count):
@@ -100,41 +107,44 @@
             cross_copy(par, c).start()
             own_copy(par, c).start()
         if first:
-            pltpu.make_async_copy(y_hbm, rv, y_sem).wait()
+            y_copy().wait()
+            eta_copy().wait()
         gradient = None
-        for step in range(count + LAG + 1):
-            if step < count:
-                cross_copy(par, step).wait_recv()
-                relay_copy(par, step).start()
-            if first and step in LATE:
+        done = 0
+        for step in range(count):
+            cross_copy(par, step).wait_recv()
+            relay_copy(par, step).start()
+            if first and step in late:
                 transpose_x(step)
-            c = step - LAG
-            if c == 0:
-                own_copy(par, None).wait_recv()
-            if 0 <= c < count:
+            arrived = chunks[step][0] + chunks[step][1]
+            while done < count and (step == count - 1 or chunks[done][0] + chunks[done][1] + RELAY_ROWS <= arrived):
+                c = done
+                done += 1
+                own_copy(par, c).wait_recv()
                 relay_copy(par, c).wait_recv()
                 rows = rows_of(c)
                 u = [ubuf[par, slot, :, rows].astype(jnp.float32) for slot in range(4)]
                 total = (u[OWN] + u[PARTNER]) + (u[CROSS] + u[RELAYED])
                 residual = rv[:, rows] - (total if first else COMBINE_WEIGHT * total)
                 rv[:, rows] = residual
-                rbuf[:, rows] = residual.astype(jnp.bfloat16)
-            if c >= 1 and not last:
-                rows = rows_of(c - 1)
-                part = jnp.dot(rbuf[:, rows], xv[rows, :], preferred_element_type=jnp.float32)
-                gradient = part if gradient is None else gradient + part
+                if not last:
+                    part = jnp.dot(residual.astype(jnp.bfloat16), xv[rows, :], preferred_element_type=jnp.float32)
+                    gradient = part if gradient is None else gradient + part
         if not last:
             update_weights(gradient)
 
+    w_copy().start()
     for c in range(count):
         x_copy(c).start()
         if c == 0:
-            pltpu.make_async_copy(y_hbm, rv, y_sem).start()
+            y_copy().start()
+            eta_copy().start()
     barrier = pltpu.get_barrier_semaphore()
     for peer in (partner, cross):
         pl.semaphore_signal(barrier, inc=1, device_id={'feat': peer}, device_id_type=MESH)
-    wv[...] = w0_ref[...]
-    dwv[...] = w0_ref[...].astype(jnp.bfloat16)
+    w_copy().wait()
+    dwv[...] = wv[...].astype(jnp.bfloat16)
+
     phase(0, first=True)
 
     def sweep(s, carry):
@@ -156,22 +166,22 @@
         lasso_weight = 0.3 * group_size / features ** 0.5
         chunks = chunk_list(samples)
         count = len(chunks)
-        any_spec = pl.BlockSpec(memory_space=pl.ANY)
+        hbm_spec = pl.BlockSpec(memory_space=pltpu.HBM)
         vmem_spec = pl.BlockSpec(memory_space=pltpu.VMEM)
         dma = pltpu.SemaphoreType.DMA
         w_t, r_t = pl.pallas_call(
             functools.partial(kernel, chunks, lasso_weight, samples),
             out_shape=(pltpu.VMEM((targets, local_features), jnp.float32), pltpu.VMEM((targets, samples), jnp.float32)),
-            in_specs=[pl.BlockSpec(memory_space=pltpu.HBM), vmem_spec, pl.BlockSpec(memory_space=pltpu.HBM), vmem_spec],
+            in_specs=[hbm_spec] * 4,
             out_specs=(vmem_spec, vmem_spec),
             scratch_shapes=[
                 pltpu.VMEM((samples, local_features), jnp.bfloat16),
                 pltpu.VMEM((samples // TILE, local_features, TILE), jnp.bfloat16),
                 pltpu.VMEM((2, 4, targets, samples), jnp.bfloat16),
-                pltpu.VMEM((targets, samples), jnp.bfloat16),
                 pltpu.VMEM((targets, local_features), jnp.bfloat16),
-                dma((count,)), dma,
-                dma((2,)), dma((2,)), dma((2,)), dma((2,)), dma((2, count)), dma((2, count)),
+                pltpu.VMEM((1, local_features), jnp.float32),
+                dma((count,)), dma((3,)),
+                dma((2, count)), dma((2, count)), dma((2, count)), dma((2, count)), dma((2, count)), dma((2, count)),
             ],
             compiler_params=pltpu.CompilerParams(collective_id=0, has_side_effects=True, vmem_limit_bytes=60 * 1024 * 1024),
             name='block_lasso',

time: 74.1 us -> 74 us (level)
  no operation moved by 1% of the time
where the time goes in v9:
time: 74 us; the launch traced here: 73.9 us
  Pallas kernels  71.9 us (97%)
  local copies, waits for them, and re-layouts  1.4 us (2%)
    pallas_call x1, Pallas kernels, local_run(): pl.pallas_call(functools.partial(kernel, chunks, lasso_weight, samples),...  71.9 us

profile of v9, /device:TPU:0, one launch (start us, length us, event | category | flops | bytes accessed | tf_op | source)
XLA Modules:
  0.0 73.9 jit_solution(4748538270824251402)
XLA Ops:
  0.6 71.9 %block_lasso.1 = (f32[8,512]{1,0:T(8,128)S(1)}, f32[8,16384]{1,0:T(8,128)S(1)}) custom-call(bf16[16384,512]{1,0:T(8,128)(2,1)} %refs_0_.1, f32[8,512]{1,0:T(8,128)} %bitcast.8, f32[8,16384]{1,0:T(8,128)} %bitcast.7, f32[1,512]{1,0:T(1,128)} %bitcast.9), custom_call_target="tpu_custom_call" | custom-call | tf_op jit(solution)/shard_map/block_lasso/pallas_call | solution.py:172
  72.5 0.6 copy.8
  73.1 0.8 %copy.9 = f32[16384,8]{0,1:T(8,128)} copy(f32[16384,8]{0,1:T(8,128)S(1)} %bitcast.5) | data formatting | bytes 1048576

commit v10 on v9

--- a/solution.py
+++ b/solution.py
@@ -16,7 +16,7 @@
 
 
 def chunk_list(samples):
-    sizes = [1024] + [2048] * (samples // 2048 - 1) + [1024]
+    sizes = [2048] * (samples // 2048)
     return [(sum(sizes[:i]), size) for i, size in enumerate(sizes)]
 
 

time: 74 us -> 73.4 us (level)
  no operation moved by 1% of the time
where the time goes in v10:
time: 73.4 us; the launch traced here: 73.2 us
  Pallas kernels  71.2 us (97%)
  local copies, waits for them, and re-layouts  1.4 us (2%)
    pallas_call x1, Pallas kernels, local_run(): pl.pallas_call(functools.partial(kernel, chunks, lasso_weight, samples),...  71.2 us

profile of v10, /device:TPU:0, one launch (start us, length us, event | category | flops | bytes accessed | tf_op | source)
XLA Modules:
  0.0 73.2 jit_solution(7891589263145413003)
XLA Ops:
  0.6 71.2 %block_lasso.1 = (f32[8,512]{1,0:T(8,128)S(1)}, f32[8,16384]{1,0:T(8,128)S(1)}) custom-call(bf16[16384,512]{1,0:T(8,128)(2,1)} %refs_0_.1, f32[8,512]{1,0:T(8,128)} %bitcast.8, f32[8,16384]{1,0:T(8,128)} %bitcast.7, f32[1,512]{1,0:T(1,128)} %bitcast.9), custom_call_target="tpu_custom_call" | custom-call | tf_op jit(solution)/shard_map/block_lasso/pallas_call | solution.py:172
  71.8 0.6 copy.8
  72.4 0.8 %copy.9 = f32[16384,8]{0,1:T(8,128)} copy(f32[16384,8]{0,1:T(8,128)S(1)} %bitcast.5) | data formatting | bytes 1048576

commit v11 on v10

--- a/solution.py
+++ b/solution.py
@@ -24,7 +24,6 @@
     (x_hbm, w0_hbm, y_hbm, eta_hbm, wv, rv, xv, xt, ubuf, dwv, eta_ref, x_sem, small_sem,
      own_send, cross_send, relay_send, own_recv, cross_recv, relay_recv) = refs
     count = len(chunks)
-    late = [c for c in range(count) if c % 2 == 1]
     me = lax.axis_index('feat')
     partner = me + 1 - 2 * lax.rem(me, 2)
     cross = 3 - me
@@ -63,21 +62,17 @@
     def relay_copy(par, c):
         return remote(par, c, CROSS, RELAYED, partner, relay_send, relay_recv)
 
-    def transpose_x(c):
-        for t in tiles_of(c):
-            xt[t] = xv[pl.ds(t * TILE, TILE), :].T
-
     def forward(par, c, first):
         change = dwv[...]
         for t in tiles_of(c):
             rows = pl.ds(t * TILE, TILE)
             if first:
-                product = lax.dot_general(change, xv[rows, :], (((1,), (1,)), ((), ())), preferred_element_type=jnp.float32)
+                x_t = xv[rows, :].T
+                xt[t] = x_t
             else:
-                product = jnp.dot(change, xt[t], preferred_element_type=jnp.float32)
+                x_t = xt[t]
+            product = jnp.dot(change, x_t, preferred_element_type=jnp.float32)
             ubuf[par, OWN, :, rows] = product.astype(jnp.bfloat16)
-        if first and c not in late:
-            transpose_x(c)
 
     def update_weights(gradient):
         eta = jnp.broadcast_to(eta_ref[...], gradient.shape)
@@ -114,8 +109,6 @@
         for step in range(count):
             cross_copy(par, step).wait_recv()
             relay_copy(par, step).start()
-            if first and step in late:
-                transpose_x(step)
             arrived = chunks[step][0] + chunks[step][1]
             while done < count and (step == count - 1 or chunks[done][0] + chunks[done][1] + RELAY_ROWS <= arrived):
                 c = done

time: 73.4 us -> 72.5 us (0.988)
  Pallas kernels: 71.2 us -> 70.4 us
    pallas_call x1, Pallas kernels: 71.2 us -> 70.4 us  [local_run(): pl.pallas_call(functools.partial(kernel, chunks, lasso_weight, samples),...]
where the time goes in v11:
time: 72.5 us; the launch traced here: 72.4 us
  Pallas kernels  70.4 us (97%)
  local copies, waits for them, and re-layouts  1.4 us (2%)
    pallas_call x1, Pallas kernels, local_run(): pl.pallas_call(functools.partial(kernel, chunks, lasso_weight, samples),...  70.4 us

profile of v11, /device:TPU:0, one launch (start us, length us, event | category | flops | bytes accessed | tf_op | source)
XLA Modules:
  0.0 72.4 jit_solution(15290018900925600893)
XLA Ops:
  0.6 70.4 %block_lasso.1 = (f32[8,512]{1,0:T(8,128)S(1)}, f32[8,16384]{1,0:T(8,128)S(1)}) custom-call(bf16[16384,512]{1,0:T(8,128)(2,1)} %refs_0_.1, f32[8,512]{1,0:T(8,128)} %bitcast.8, f32[8,16384]{1,0:T(8,128)} %bitcast.7, f32[1,512]{1,0:T(1,128)} %bitcast.9), custom_call_target="tpu_custom_call" | custom-call | tf_op jit(solution)/shard_map/block_lasso/pallas_call | solution.py:165
  71.0 0.6 copy.8
  71.6 0.8 %copy.9 = f32[16384,8]{0,1:T(8,128)} copy(f32[16384,8]{0,1:T(8,128)S(1)} %bitcast.5) | data formatting | bytes 1048576

commit v12 on v6

--- a/solution.py
+++ b/solution.py
@@ -89,6 +89,8 @@
             forward(par, c, first)
             if c == count // 2 and not first:
                 wait_sends(1 - par)
+            if first and c == 0:
+                pl.semaphore_wait(barrier, 2)
             cross_copy(par, c).start()
             own_copy(par, c).start()
         if first:
@@ -123,8 +125,6 @@
         pl.semaphore_signal(barrier, inc=1, device_id={'feat': peer}, device_id_type=MESH)
     wv[...] = w0_ref[...]
     dwv[...] = w0_ref[...].astype(jnp.bfloat16)
-    pl.semaphore_wait(barrier, 2)
-
     phase(0, first=True)
 
     def sweep(s, carry):
@@ -134,6 +134,14 @@
     lax.fori_loop(1, SWEEPS, sweep, 0)
     phase(SWEEPS % 2, last=True)
     wait_sends(SWEEPS % 2)
+
+
+def leave(w_ref, r_ref, w_hbm, r_hbm, sem):
+    copies = [pltpu.make_async_copy(w_ref, w_hbm, sem.at[0]), pltpu.make_async_copy(r_ref, r_hbm, sem.at[1])]
+    for copy in copies:
+        copy.start()
+    for copy in copies:
+        copy.wait()
 
 
 def solution(mesh):
@@ -165,6 +173,14 @@
             compiler_params=pltpu.CompilerParams(collective_id=0, has_side_effects=True, vmem_limit_bytes=60 * 1024 * 1024),
             name='block_lasso',
         )(x_local, coef_local.T, targets_local.T, step_local[None, :])
+        w_t, r_t = pl.pallas_call(
+            leave,
+            out_shape=(jax.ShapeDtypeStruct(w_t.shape, w_t.dtype), jax.ShapeDtypeStruct(r_t.shape, r_t.dtype)),
+            in_specs=[vmem_spec, vmem_spec],
+            out_specs=(any_spec, any_spec),
+            scratch_shapes=[dma((2,))],
+            name='leave',
+        )(w_t, r_t)
         return w_t.T, r_t.T
 
     return jax.shard_map(local_run, mesh=mesh, in_specs=(P('prob', 'feat'), P(('prob', 'feat'), None), P('prob', None), P(('prob', 'feat'))), out_specs=(P(('prob', 'feat'), None), P('prob', None)), check_vma=False)

time: 71.1 us -> 73.2 us (1.030)
  Pallas kernels: 68.9 us -> 70.8 us
    pallas_call x0 -> x1, Pallas kernels: none -> 1.87 us  [local_run(): pl.pallas_call(leave, out_shape=(jax.ShapeDtypeStruct(w_t.shape, w_t.dtyp...]
where the time goes in v12:
time: 73.2 us; the launch traced here: 72.9 us
  Pallas kernels  70.8 us (97%)
  local copies, waits for them, and re-layouts  1.38 us (2%)
  between operations  0.81 us (1%)
    pallas_call x1, Pallas kernels, local_run(): pl.pallas_call(functools.partial(kernel, chunks, lasso_weight, samples),...  68.9 us
    pallas_call x1, Pallas kernels, local_run(): pl.pallas_call(leave, out_shape=(jax.ShapeDtypeStruct(w_t.shape, w_t.dtyp...  1.87 us

profile of v12, /device:TPU:0, one launch (start us, length us, event | category | flops | bytes accessed | tf_op | source)
XLA Modules:
  0.0 72.9 jit_solution(2821185146109193070)
XLA Ops:
  0.6 68.9 %block_lasso.1 = (f32[8,512]{1,0:T(8,128)S(1)}, f32[8,16384]{1,0:T(8,128)S(1)}) custom-call(bf16[16384,512]{1,0:T(8,128)(2,1)} %refs_0_.1, f32[8,512]{1,0:T(8,128)} %bitcast.6, f32[8,16384]{1,0:T(8,128)} %bitcast.5, f32[1,512]{1,0:T(1,128)} %bitcast.7), custom_call_target="tpu_custom_call" | custom-call | tf_op jit(solution)/shard_map/block_lasso/pallas_call | solution.py:160
  69.5 0.0 copy-start
  69.5 0.8 %copy-done = f32[8,16384]{1,0:T(8,128)} copy-done((f32[8,16384]{1,0:T(8,128)}, f32[8,16384]{1,0:T(8,128)S(1)}, u32[]{:S(2)}) %copy-start) | copy-done | bytes 524312
  70.3 0.0 copy-start.1
  70.3 0.6 copy-done.1
  70.9 1.9 %leave.1 = (f32[8,512]{1,0:T(8,128)}, f32[8,16384]{1,0:T(8,128)}) custom-call(f32[8,512]{1,0:T(8,128)} %copy-done.1, f32[8,16384]{1,0:T(8,128)} %copy-done), custom_call_target="tpu_custom_call" | custom-call | tf_op jit(solution)/shard_map/leave/pallas_call | solution.py:176
Async XLA Ops:
  69.5 0.8 %copy-start = (f32[8,16384]{1,0:T(8,128)}, f32[8,16384]{1,0:T(8,128)S(1)}, u32[]{:S(2)}) copy-start(f32[8,16384]{1,0:T(8,128)S(1)} %get-tuple-element.7.r_ref) | copy-start | bytes 1572868
  70.3 0.6 copy-start.1

commit v13 on v6

--- a/solution.py
+++ b/solution.py
@@ -59,11 +59,10 @@
         for t in tiles_of(c):
             rows = pl.ds(t * TILE, TILE)
             if first:
-                x_t = xv[rows, :].T
-                xt[t] = x_t
+                product = lax.dot_general(change, xv[rows, :], (((1,), (1,)), ((), ())), preferred_element_type=jnp.float32)
+                xt[t] = xv[rows, :].T
             else:
-                x_t = xt[t]
-            product = jnp.dot(change, x_t, preferred_element_type=jnp.float32)
+                product = jnp.dot(change, xt[t], preferred_element_type=jnp.float32)
             ubuf[par, OWN, :, rows] = product.astype(jnp.bfloat16)
 
     def update_weights(gradient):

time: 71.1 us -> 70.9 us (level)
  no operation moved by 1% of the time
where the time goes in v13:
time: 70.9 us; the launch traced here: 70.6 us
  Pallas kernels  68.6 us (97%)
  local copies, waits for them, and re-layouts  1.4 us (2%)
    pallas_call x1, Pallas kernels, local_run(): pl.pallas_call(functools.partial(kernel, chunks, lasso_weight, samples),...  68.6 us

profile of v13, /device:TPU:0, one launch (start us, length us, event | category | flops | bytes accessed | tf_op | source)
XLA Modules:
  0.0 70.6 jit_solution(4259777870178200320)
XLA Ops:
  0.6 68.6 %block_lasso.1 = (f32[8,512]{1,0:T(8,128)S(1)}, f32[8,16384]{1,0:T(8,128)S(1)}) custom-call(bf16[16384,512]{1,0:T(8,128)(2,1)} %refs_0_.1, f32[8,512]{1,0:T(8,128)} %bitcast.8, f32[8,16384]{1,0:T(8,128)} %bitcast.7, f32[1,512]{1,0:T(1,128)} %bitcast.9), custom_call_target="tpu_custom_call" | custom-call | tf_op jit(solution)/shard_map/block_lasso/pallas_call | solution.py:151
  69.2 0.6 copy.8
  69.8 0.8 %copy.9 = f32[16384,8]{0,1:T(8,128)} copy(f32[16384,8]{0,1:T(8,128)S(1)} %bitcast.5) | data formatting | bytes 1048576

commit v14 on v13

--- a/solution.py
+++ b/solution.py
@@ -16,8 +16,8 @@
 
 
 def chunk_list(samples):
-    size = samples // 8
-    return [(i * size, size) for i in range(8)]
+    sizes = [2048] * (samples // 2048 - 1) + [1024, 1024]
+    return [(sum(sizes[:i]), size) for i, size in enumerate(sizes)]
 
 
 def kernel(chunks, lasso_weight, samples, *refs):
@@ -115,8 +115,7 @@
 
     for c in range(count):
         x_copy(c).start()
-        if c == 0:
-            pltpu.make_async_copy(y_hbm, rv, y_sem).start()
+    pltpu.make_async_copy(y_hbm, rv, y_sem).start()
     barrier = pltpu.get_barrier_semaphore()
     for peer in (partner, cross):
         pl.semaphore_signal(barrier, inc=1, device_id={'feat': peer}, device_id_type=MESH)

time: 70.9 us -> 73.2 us (1.032)
  Pallas kernels: 68.6 us -> 70.9 us
    pallas_call x1, Pallas kernels: 68.6 us -> 70.9 us  [local_run(): pl.pallas_call(functools.partial(kernel, chunks, lasso_weight, samples),...]
where the time goes in v14:
time: 73.2 us; the launch traced here: 73 us
  Pallas kernels  70.9 us (97%)
  local copies, waits for them, and re-layouts  1.4 us (2%)
    pallas_call x1, Pallas kernels, local_run(): pl.pallas_call(functools.partial(kernel, chunks, lasso_weight, samples),...  70.9 us

profile of v14, /device:TPU:0, one launch (start us, length us, event | category | flops | bytes accessed | tf_op | source)
XLA Modules:
  0.0 73.0 jit_solution(12234540345621733973)
XLA Ops:
  0.6 70.9 %block_lasso.1 = (f32[8,512]{1,0:T(8,128)S(1)}, f32[8,16384]{1,0:T(8,128)S(1)}) custom-call(bf16[16384,512]{1,0:T(8,128)(2,1)} %refs_0_.1, f32[8,512]{1,0:T(8,128)} %bitcast.8, f32[8,16384]{1,0:T(8,128)} %bitcast.7, f32[1,512]{1,0:T(1,128)} %bitcast.9), custom_call_target="tpu_custom_call" | custom-call | tf_op jit(solution)/shard_map/block_lasso/pallas_call | solution.py:150
  71.6 0.6 copy.8
  72.2 0.8 %copy.9 = f32[16384,8]{0,1:T(8,128)} copy(f32[16384,8]{0,1:T(8,128)S(1)} %bitcast.5) | data formatting | bytes 1048576

commit v15 on v13

--- a/solution.py
+++ b/solution.py
@@ -10,6 +10,7 @@
 SWEEPS = 6
 COMBINE_WEIGHT = 0.8
 LAG = 2
+IN_FLIGHT = 2
 TILE = 256
 MESH = pl.DeviceIdType.MESH
 OWN, PARTNER, CROSS, RELAYED = 0, 1, 2, 3
@@ -78,7 +79,8 @@
     def wait_sends(par):
         for c in range(count):
             own_copy(par, c).wait_send()
-            cross_copy(par, c).wait_send()
+            if c >= count - IN_FLIGHT:
+                cross_copy(par, c).wait_send()
             relay_copy(par, c).wait_send()
 
     def phase(par, first=False, last=False):
@@ -88,6 +90,8 @@
             forward(par, c, first)
             if c == count // 2 and not first:
                 wait_sends(1 - par)
+            if c >= IN_FLIGHT:
+                cross_copy(par, c - IN_FLIGHT).wait_send()
             cross_copy(par, c).start()
             own_copy(par, c).start()
         if first:

time: 70.9 us -> 79.2 us (1.12)
  Pallas kernels: 68.6 us -> 76.9 us
    pallas_call x1, Pallas kernels: 68.6 us -> 76.9 us  [local_run(): pl.pallas_call(functools.partial(kernel, chunks, lasso_weight, samples),...]
where the time goes in v15:
time: 79.2 us; the launch traced here: 78.9 us
  Pallas kernels  76.9 us (97%)
  local copies, waits for them, and re-layouts  1.4 us (2%)
    pallas_call x1, Pallas kernels, local_run(): pl.pallas_call(functools.partial(kernel, chunks, lasso_weight, samples),...  76.9 us

profile of v15, /device:TPU:0, one launch (start us, length us, event | category | flops | bytes accessed | tf_op | source)
XLA Modules:
  0.0 78.9 jit_solution(13086089531855484670)
XLA Ops:
  0.6 76.9 %block_lasso.1 = (f32[8,512]{1,0:T(8,128)S(1)}, f32[8,16384]{1,0:T(8,128)S(1)}) custom-call(bf16[16384,512]{1,0:T(8,128)(2,1)} %refs_0_.1, f32[8,512]{1,0:T(8,128)} %bitcast.8, f32[8,16384]{1,0:T(8,128)} %bitcast.7, f32[1,512]{1,0:T(1,128)} %bitcast.9), custom_call_target="tpu_custom_call" | custom-call | tf_op jit(solution)/shard_map/block_lasso/pallas_call | solution.py:155
  77.5 0.6 copy.8
  78.1 0.8 %copy.9 = f32[16384,8]{0,1:T(8,128)} copy(f32[16384,8]{0,1:T(8,128)S(1)} %bitcast.5) | data formatting | bytes 1048576

commit v16 on v13

--- a/solution.py
+++ b/solution.py
@@ -37,8 +37,10 @@
         start, size = chunks[c]
         return range(start // TILE, (start + size) // TILE)
 
-    def x_copy(c):
-        return pltpu.make_async_copy(x_hbm.at[rows_of(c)], xv.at[rows_of(c)], x_sem.at[c])
+    def x_copy(c, half):
+        start, size = chunks[c]
+        rows = pl.ds(start + half * (size // 2), size // 2)
+        return pltpu.make_async_copy(x_hbm.at[rows], xv.at[rows], x_sem.at[c, half])
 
     def remote(par, c, src, dst, peer, send_sem, recv_sem):
         return pltpu.make_async_remote_copy(
@@ -56,8 +58,10 @@
 
     def forward(par, c, first):
         change = dwv[...]
-        for t in tiles_of(c):
+        for i, t in enumerate(tiles_of(c)):
             rows = pl.ds(t * TILE, TILE)
+            if first and 2 * i % len(tiles_of(c)) == 0:
+                x_copy(c, 2 * i // len(tiles_of(c))).wait()
             if first:
                 product = lax.dot_general(change, xv[rows, :], (((1,), (1,)), ((), ())), preferred_element_type=jnp.float32)
                 xt[t] = xv[rows, :].T
@@ -83,8 +87,6 @@
 
     def phase(par, first=False, last=False):
         for c in range(count):
-            if first:
-                x_copy(c).wait()
             forward(par, c, first)
             if c == count // 2 and not first:
                 wait_sends(1 - par)
@@ -114,7 +116,8 @@
             update_weights(gradient)
 
     for c in range(count):
-        x_copy(c).start()
+        x_copy(c, 0).start()
+        x_copy(c, 1).start()
         if c == 0:
             pltpu.make_async_copy(y_hbm, rv, y_sem).start()
     barrier = pltpu.get_barrier_semaphore()
@@ -133,6 +136,14 @@
     lax.fori_loop(1, SWEEPS, sweep, 0)
     phase(SWEEPS % 2, last=True)
     wait_sends(SWEEPS % 2)
+
+
+def leave(w_ref, r_ref, w_hbm, r_hbm, sem):
+    copies = [pltpu.make_async_copy(r_ref, r_hbm, sem.at[1]), pltpu.make_async_copy(w_ref, w_hbm, sem.at[0])]
+    for copy in copies:
+        copy.start()
+    for copy in copies:
+        copy.wait()
 
 
 def solution(mesh):
@@ -158,12 +169,20 @@
                 pltpu.VMEM((samples // TILE, local_features, TILE), jnp.bfloat16),
                 pltpu.VMEM((2, 4, targets, samples), jnp.bfloat16),
                 pltpu.VMEM((targets, local_features), jnp.bfloat16),
-                dma((count,)), dma,
+                dma((count, 2)), dma,
                 dma((2, count)), dma((2, count)), dma((2, count)), dma((2, count)), dma((2, count)), dma((2, count)),
             ],
             compiler_params=pltpu.CompilerParams(collective_id=0, has_side_effects=True, vmem_limit_bytes=60 * 1024 * 1024),
             name='block_lasso',
         )(x_local, coef_local.T, targets_local.T, step_local[None, :])
+        w_t, r_t = pl.pallas_call(
+            leave,
+            out_shape=(jax.ShapeDtypeStruct(w_t.shape, w_t.dtype), jax.ShapeDtypeStruct(r_t.shape, r_t.dtype)),
+            in_specs=[vmem_spec, vmem_spec],
+            out_specs=(any_spec, any_spec),
+            scratch_shapes=[dma((2,))],
+            name='leave',
+        )(pltpu.with_memory_space_constraint(w_t, pltpu.VMEM), pltpu.with_memory_space_constraint(r_t, pltpu.VMEM))
         return w_t.T, r_t.T
 
     return jax.shard_map(local_run, mesh=mesh, in_specs=(P('prob', 'feat'), P(('prob', 'feat'), None), P('prob', None), P(('prob', 'feat'))), out_specs=(P(('prob', 'feat'), None), P('prob', None)), check_vma=False)

time: 70.9 us -> 71.1 us (level)
  Pallas kernels: 68.6 us -> 70 us
  local copies, waits for them, and re-layouts: 1.4 us -> 0 us
    unnamed x2 -> x0, local copies, waits for them, and re-layouts: 1.4 us -> none
    pallas_call x0 -> x1, Pallas kernels: none -> 0.81 us  [local_run(): pl.pallas_call(leave, out_shape=(jax.ShapeDtypeStruct(w_t.shape, w_t.dtyp...]
where the time goes in v16:
time: 71.1 us; the launch traced here: 70.8 us
  Pallas kernels  70 us (98%)
  between operations  0.8 us (1%)
    pallas_call x1, Pallas kernels, local_run(): pl.pallas_call(functools.partial(kernel, chunks, lasso_weight, samples),...  69.2 us

profile of v16, /device:TPU:0, one launch (start us, length us, event | category | flops | bytes accessed | tf_op | source)
XLA Modules:
  0.0 70.8 jit_solution(14633619361319230032)
XLA Ops:
  0.6 69.2 %block_lasso.1 = (f32[8,512]{1,0:T(8,128)S(1)}, f32[8,16384]{1,0:T(8,128)S(1)}) custom-call(bf16[16384,512]{1,0:T(8,128)(2,1)} %refs_0_.1, f32[8,512]{1,0:T(8,128)} %bitcast.6, f32[8,16384]{1,0:T(8,128)} %bitcast.5, f32[1,512]{1,0:T(1,128)} %bitcast.7), custom_call_target="tpu_custom_call" | custom-call | tf_op jit(solution)/shard_map/block_lasso/pallas_call | solution.py:162
  69.9 0.8 %leave.1 = (f32[8,512]{1,0:T(8,128)}, f32[8,16384]{1,0:T(8,128)}) custom-call(f32[8,512]{1,0:T(8,128)S(1)} %get-tuple-element.6.w_ref, f32[8,16384]{1,0:T(8,128)S(1)} %get-tuple-element.7.r_ref), custom_call_target="tpu_custom_call" | custom-call | tf_op jit(solution)/shard_map/leave/pallas_call | solution.py:178

commit v17 on v13

--- a/solution.py
+++ b/solution.py
@@ -135,6 +135,14 @@
     wait_sends(SWEEPS % 2)
 
 
+def leave(w_ref, r_ref, w_hbm, r_hbm, sem):
+    copies = [pltpu.make_async_copy(r_ref, r_hbm, sem.at[1]), pltpu.make_async_copy(w_ref, w_hbm, sem.at[0])]
+    for copy in copies:
+        copy.start()
+    for copy in copies:
+        copy.wait()
+
+
 def solution(mesh):
     group_size = mesh.shape['feat']
 
@@ -164,6 +172,14 @@
             compiler_params=pltpu.CompilerParams(collective_id=0, has_side_effects=True, vmem_limit_bytes=60 * 1024 * 1024),
             name='block_lasso',
         )(x_local, coef_local.T, targets_local.T, step_local[None, :])
+        w_t, r_t = pl.pallas_call(
+            leave,
+            out_shape=(jax.ShapeDtypeStruct(w_t.shape, w_t.dtype), jax.ShapeDtypeStruct(r_t.shape, r_t.dtype)),
+            in_specs=[vmem_spec, vmem_spec],
+            out_specs=(any_spec, any_spec),
+            scratch_shapes=[dma((2,))],
+            name='leave',
+        )(pltpu.with_memory_space_constraint(w_t, pltpu.VMEM), pltpu.with_memory_space_constraint(r_t, pltpu.VMEM))
         return w_t.T, r_t.T
 
     return jax.shard_map(local_run, mesh=mesh, in_specs=(P('prob', 'feat'), P(('prob', 'feat'), None), P('prob', None), P(('prob', 'feat'))), out_specs=(P(('prob', 'feat'), None), P('prob', None)), check_vma=False)

time: 70.9 us -> 70.4 us (level)
  local copies, waits for them, and re-layouts: 1.4 us -> 0 us
  Pallas kernels: 68.6 us -> 69.4 us
    unnamed x2 -> x0, local copies, waits for them, and re-layouts: 1.4 us -> none
    pallas_call x0 -> x1, Pallas kernels: none -> 0.81 us  [local_run(): pl.pallas_call(leave, out_shape=(jax.ShapeDtypeStruct(w_t.shape, w_t.dtyp...]
where the time goes in v17:
time: 70.4 us; the launch traced here: 70.2 us
  Pallas kernels  69.4 us (99%)
  between operations  0.8 us (1%)
    pallas_call x1, Pallas kernels, local_run(): pl.pallas_call(functools.partial(kernel, chunks, lasso_weight, samples),...  68.6 us

profile of v17, /device:TPU:0, one launch (start us, length us, event | category | flops | bytes accessed | tf_op | source)
XLA Modules:
  0.0 70.2 jit_solution(2253704925552351236)
XLA Ops:
  0.6 68.6 %block_lasso.1 = (f32[8,512]{1,0:T(8,128)S(1)}, f32[8,16384]{1,0:T(8,128)S(1)}) custom-call(bf16[16384,512]{1,0:T(8,128)(2,1)} %refs_0_.1, f32[8,512]{1,0:T(8,128)} %bitcast.6, f32[8,16384]{1,0:T(8,128)} %bitcast.5, f32[1,512]{1,0:T(1,128)} %bitcast.7), custom_call_target="tpu_custom_call" | custom-call | tf_op jit(solution)/shard_map/block_lasso/pallas_call | solution.py:159
  69.2 0.8 %leave.1 = (f32[8,512]{1,0:T(8,128)}, f32[8,16384]{1,0:T(8,128)}) custom-call(f32[8,512]{1,0:T(8,128)S(1)} %get-tuple-element.6.w_ref, f32[8,16384]{1,0:T(8,128)S(1)} %get-tuple-element.7.r_ref), custom_call_target="tpu_custom_call" | custom-call | tf_op jit(solution)/shard_map/leave/pallas_call | solution.py:175

commit v18 on v17

--- a/solution.py
+++ b/solution.py
@@ -16,8 +16,8 @@
 
 
 def chunk_list(samples):
-    size = samples // 8
-    return [(i * size, size) for i in range(8)]
+    sizes = [1024, 1024] + [2048] * (samples // 2048 - 1)
+    return [(sum(sizes[:i]), size) for i, size in enumerate(sizes)]
 
 
 def kernel(chunks, lasso_weight, samples, *refs):

time: 70.4 us -> 71.6 us (1.017)
  Pallas kernels: 69.4 us -> 70.6 us
    pallas_call x1, Pallas kernels: 68.6 us -> 69.7 us  [local_run(): pl.pallas_call(functools.partial(kernel, chunks, lasso_weight, samples),...]
where the time goes in v18:
time: 71.6 us; the launch traced here: 71.4 us
  Pallas kernels  70.6 us (99%)
  between operations  0.8 us (1%)
    pallas_call x1, Pallas kernels, local_run(): pl.pallas_call(functools.partial(kernel, chunks, lasso_weight, samples),...  69.7 us

profile of v18, /device:TPU:0, one launch (start us, length us, event | category | flops | bytes accessed | tf_op | source)
XLA Modules:
  0.0 71.4 jit_solution(10408882342602229527)
XLA Ops:
  0.6 69.7 %block_lasso.1 = (f32[8,512]{1,0:T(8,128)S(1)}, f32[8,16384]{1,0:T(8,128)S(1)}) custom-call(bf16[16384,512]{1,0:T(8,128)(2,1)} %refs_0_.1, f32[8,512]{1,0:T(8,128)} %bitcast.6, f32[8,16384]{1,0:T(8,128)} %bitcast.5, f32[1,512]{1,0:T(1,128)} %bitcast.7), custom_call_target="tpu_custom_call" | custom-call | tf_op jit(solution)/shard_map/block_lasso/pallas_call | solution.py:159
  70.4 0.8 %leave.1 = (f32[8,512]{1,0:T(8,128)}, f32[8,16384]{1,0:T(8,128)}) custom-call(f32[8,512]{1,0:T(8,128)S(1)} %get-tuple-element.6.w_ref, f32[8,16384]{1,0:T(8,128)S(1)} %get-tuple-element.7.r_ref), custom_call_target="tpu_custom_call" | custom-call | tf_op jit(solution)/shard_map/leave/pallas_call | solution.py:175

commit v19 on v18

--- a/solution.py
+++ b/solution.py
@@ -16,7 +16,7 @@
 
 
 def chunk_list(samples):
-    sizes = [1024, 1024] + [2048] * (samples // 2048 - 1)
+    sizes = [2048] + [3072] * ((samples - 4096) // 3072) + [2048]
     return [(sum(sizes[:i]), size) for i, size in enumerate(sizes)]
 
 

time: 71.6 us -> 72.4 us (1.011)
  Pallas kernels: 70.6 us -> 71.6 us
    pallas_call x1, Pallas kernels: 69.7 us -> 70.7 us  [local_run(): pl.pallas_call(functools.partial(kernel, chunks, lasso_weight, samples),...]
where the time goes in v19:
time: 72.4 us; the launch traced here: 72.2 us
  Pallas kernels  71.6 us (99%)
    pallas_call x1, Pallas kernels, local_run(): pl.pallas_call(functools.partial(kernel, chunks, lasso_weight, samples),...  70.7 us

profile of v19, /device:TPU:0, one launch (start us, length us, event | category | flops | bytes accessed | tf_op | source)
XLA Modules:
  0.0 72.2 jit_solution(10160161625520573833)
XLA Ops:
  0.6 70.7 %block_lasso.1 = (f32[8,512]{1,0:T(8,128)S(1)}, f32[8,16384]{1,0:T(8,128)S(1)}) custom-call(bf16[16384,512]{1,0:T(8,128)(2,1)} %refs_0_.1, f32[8,512]{1,0:T(8,128)} %bitcast.6, f32[8,16384]{1,0:T(8,128)} %bitcast.5, f32[1,512]{1,0:T(1,128)} %bitcast.7), custom_call_target="tpu_custom_call" | custom-call | tf_op jit(solution)/shard_map/block_lasso/pallas_call | solution.py:159
  71.4 0.8 %leave.1 = (f32[8,512]{1,0:T(8,128)}, f32[8,16384]{1,0:T(8,128)}) custom-call(f32[8,512]{1,0:T(8,128)S(1)} %get-tuple-element.6.w_ref, f32[8,16384]{1,0:T(8,128)S(1)} %get-tuple-element.7.r_ref), custom_call_target="tpu_custom_call" | custom-call | tf_op jit(solution)/shard_map/leave/pallas_call | solution.py:175
